TPU v7x, 128 devices: a whole 4x4x4 slice. The times are simulated.
128 devices in a mesh: seq: 16 (over z, y_hi, core), fsdp: 8 (over y_lo, x).
Axes of the slice: x: 4, y: 4 (y_hi: 2, y_lo: 2; y = y_hi * 2 + y_lo), z: 4, core: 2. Of those that a mesh axis runs over, the one named last changes fastest.
Arguments:
- patches: bfloat16 [8, 2048, 3072], P('fsdp', 'seq'), may hold values from -6 to 6
- weight_codes: int32 [3072, 3072], P('fsdp'), may hold values from -448 to 448
- block_scales: float32 [24, 24], P('fsdp'), may hold values from 2.5e-05 to 0.0001
- key_proj: bfloat16 [8, 2048, 3072], P('fsdp', 'seq'), may hold values from -6 to 6
- value_proj: bfloat16 [8, 2048, 3072], P('fsdp', 'seq'), may hold values from -6 to 6
- query_gain: float32 [3072], replicated, may hold values from 1 to 10
- key_gain: float32 [3072], replicated, may hold values from 1 to 10
Outputs:
- attended: bfloat16 [8, 2048, 3072], P('fsdp', 'seq')
All inputs are finite; a program needn't handle non-finite values.
Results may differ from a plain program's by a relative error of at most 0.007.
The roundings to bfloat16 on the way count: a program that leaves them out, or rounds other values in their place, can miss the bound.
Values may be sent and summed in bfloat16 or wider, within the bound.
No kernel may reach another device: no remote copies, remote signals or barrier semaphores. Data moves between devices by JAX's collectives and lax.ppermute only.
A program may use at most 192 MiB of HBM per device.

v0:
```python
import math

import jax
import jax.numpy as jnp
from jax import lax
from jax.sharding import Mesh
from jax.sharding import PartitionSpec as P

HEADS = 48
HDIM = 64
BLOCK = 128
SEQ = ("seq_0", "seq_1", "seq_2")


NORM_FLOOR = 0.25


def split_up(array, dim, devices):
    before, after = (array.shape[:dim], array.shape[dim + 1 :])
    return jnp.moveaxis(array.reshape(*before, devices, -1, *after), dim, 0)


def laid_out(tiles, dim):
    tiles = jnp.moveaxis(tiles, 0, dim)
    lengths = tiles.shape
    return tiles.reshape(*lengths[:dim], lengths[dim] * lengths[dim + 1], *lengths[dim + 2 :])


def exchange_in_order(tiles, axes, order):
    inside = tiles.shape[1:]
    whole = tiles.reshape(*(lax.axis_size(a) for a in axes), *inside)
    for k in order:
        whole = lax.all_to_all(whole, axes[k], k, k, tiled=True)
    return whole.reshape(-1, *inside)


def two_step_exchange(array, groups, order, split_dim, concat_dim):
    devices = lax.axis_size(groups[0]) * lax.axis_size(groups[1])
    tiles = split_up(array, split_dim, devices)
    return laid_out(exchange_in_order(tiles, groups, order), concat_dim)


def head_norm(projected, gain_row):
    shaped = projected.reshape(projected.shape[:-1] + (HEADS, HDIM))
    average = jnp.mean(shaped, axis=-1, keepdims=True)
    centred = shaped - average
    spread = jnp.mean(centred * centred, axis=-1, keepdims=True)
    normed = centred * lax.rsqrt(spread + NORM_FLOOR) * gain_row.reshape(HEADS, HDIM)
    return normed.astype(jnp.bfloat16)


def dequantize(weight_codes, block_scales):
    row_count, column_count = weight_codes.shape
    blocked = weight_codes.astype(jnp.float32).reshape(
        row_count // BLOCK, BLOCK, column_count // BLOCK, BLOCK
    )
    return (
        (blocked * block_scales[:, None, :, None])
        .reshape(row_count, column_count)
        .astype(jnp.bfloat16)
    )


def start_of(query_view):
    image_count, token_count, head_count = (
        query_view.shape[0],
        query_view.shape[1],
        query_view.shape[2],
    )
    return (
        jnp.full((image_count, token_count, head_count), -1e30, jnp.float32),
        jnp.zeros((image_count, token_count, head_count), jnp.float32),
        jnp.zeros(query_view.shape, jnp.float32),
    )


def attend_block(query_view, state_now, key_view, value_view):
    running_max, running_sum, weighted = state_now
    scores = jnp.einsum(
        "ithd,ishd->iths", query_view, key_view, preferred_element_type=jnp.float32
    ) * HDIM ** (-0.5)
    newest = jnp.maximum(running_max, jnp.max(scores, axis=-1))
    probability = jnp.exp(scores - newest[..., None])
    running_sum = jnp.sum(probability, axis=-1)
    blended = jnp.einsum(
        "iths,ishd->ithd",
        probability.astype(jnp.bfloat16),
        value_view,
        preferred_element_type=jnp.float32,
    )
    weighted = blended
    return (newest, running_sum, weighted)


def attend_whole(members):
    query_all, key_all, value_all = members
    image_count, length, head_count, head_size = query_all.shape
    block_rows = math.gcd(length, 512)
    block_count = length // block_rows
    blocked = jnp.moveaxis(
        query_all.reshape(image_count, block_count, block_rows, head_count, head_size), 1, 0
    )

    def one_block(query_block):
        finished = attend_block(query_block, start_of(query_block), key_all, value_all)
        return (finished[2] / finished[1][..., None]).astype(jnp.bfloat16)

    outputs = lax.map(one_block, blocked)
    return jnp.moveaxis(outputs, 0, 1).reshape(image_count, length, head_count, head_size)


def per_device(patches, weight_codes, block_scales, key_proj, value_proj, query_gain, key_gain):
    image_count, token_count, feature_count = patches.shape
    flat_rows = patches.reshape(image_count * token_count, feature_count)
    key_norm = head_norm(key_proj.astype(jnp.float32), key_gain)
    value_view = value_proj.reshape(image_count, token_count, HEADS, HDIM)
    local_weight = dequantize(weight_codes, block_scales)
    group_rows = lax.all_to_all(flat_rows, "fsdp", split_axis=1, concat_axis=0, tiled=True)
    queries = lax.psum_scatter(
        jnp.dot(group_rows, local_weight, preferred_element_type=jnp.float32),
        "fsdp",
        scatter_dimension=0,
        tiled=True,
    )
    query_view = head_norm(queries, query_gain).reshape(image_count, token_count, HEADS, HDIM)
    mixed = attend_whole(
        (
            lax.all_to_all(query_view, SEQ, split_axis=2, concat_axis=1, tiled=True),
            lax.all_to_all(key_norm, SEQ, split_axis=2, concat_axis=1, tiled=True),
            lax.all_to_all(value_view, SEQ, split_axis=2, concat_axis=1, tiled=True),
        )
    )
    back = two_step_exchange(mixed, (("seq_0", "seq_1"), "seq_2"), (1, 0), 1, 2)
    return back.reshape(image_count, token_count, HEADS * HDIM)


def solution(mesh):
    split = Mesh(
        mesh.devices.reshape(4, 2, 2, mesh.shape["fsdp"]), ("seq_0", "seq_1", "seq_2", "fsdp")
    )
    placed = (
        P("fsdp", SEQ, None),
        P("fsdp", None),
        P("fsdp", None),
        P("fsdp", SEQ, None),
        P("fsdp", SEQ, None),
        P(),
        P(),
    )
    return jax.shard_map(
        per_device, mesh=split, in_specs=placed, out_specs=P("fsdp", SEQ, None), check_vma=False
    )
```

profile of v0, /device:TPU:1, one launch (start us, length us, event | category | flops | bytes accessed | tf_op | source)
XLA Modules:
  0.0 281.7 jit_solution(18361344485200395477)
XLA Ops:
  8.1 17.7 %all_to_all.80 = bf16[128,8,384]{0,2,1:T(8,128)(2,1)S(1)} all-to-all(bf16[128,8,384]{0,2,1:T(8,128)(2,1)S(1)} %bitcast.155), channel_id=1, replica_groups=mesh['seq_0'=4,'seq_1'=2,'seq_2'=2,'fsdp'=8] {'fsdp'}, dimensions={1} | all-to-all | bytes 1572864 | tf_op jit(solution)/shard_map/all_to_all | solution.py:118
  26.5 2.0 copy-done.1
  28.5 7.1 %convolution_bitcast_fusion = f32[1024,3072]{0,1:T(8,128)} fusion(bf16[1024,384]{1,0:T(8,128)(2,1)S(1)} %bitcast.148, f32[48,8,24,128]{3,2,1,0:T(8,128)S(1)} %bitcast.144, s32[384,3072]{1,0:T(8,128)S(1)} %copy-done.1), kind=kOutput, calls=%fused_computation.20 | convolution fusion | flops 2419458048 | bytes 22806528 | tf_op jit(solution)/shard_map/dot_general | solution.py:120
  39.1 9.5 %all-to-all-start.2 = ((bf16[1,128,48,64]{1,3,0,2:T(8,128)(2,1)}), bf16[1,128,48,64]{1,3,0,2:T(8,128)(2,1)S(1)}, u32[]{:S(2)}, u32[]{:S(2)}) async-start(bf16[1,128,48,64]{1,3,0,2:T(8,128)(2,1)} %fusion.30), calls=%async_computation.3 | async-start | bytes 1572864 | tf_op jit(solution)/shard_map/all_to_all | solution.py:129
  49.8 119.5 %reduce-scatter.2.cloned.1.call-done = f32[128,3072]{0,1:T(8,128)} async-done(((f32[1024,3072]{0,1:T(8,128)}), f32[128,3072]{0,1:T(8,128)}) %reduce-scatter.2.cloned.1.call-update) | async-done | bytes 1572880 | tf_op jit(solution)/shard_map/reduce_scatter | solution.py:119
  171.0 9.2 %all-to-all-done.2 = bf16[1,128,48,64]{1,3,0,2:T(8,128)(2,1)S(1)} async-done(((bf16[1,128,48,64]{1,3,0,2:T(8,128)(2,1)}), bf16[1,128,48,64]{1,3,0,2:T(8,128)(2,1)S(1)}, u32[]{:S(2)}, u32[]{:S(2)}) %all-to-all-start.2) | async-done | bytes 786464 | tf_op jit(solution)/shard_map/all_to_all | solution.py:129
  180.2 3.9 %all-to-all-start.3 = ((bf16[1,128,48,64]{1,3,0,2:T(8,128)(2,1)}), bf16[1,128,48,64]{1,3,0,2:T(8,128)(2,1)S(1)}, u32[]{:S(2)}, u32[]{:S(2)}) async-start(bf16[1,128,48,64]{1,3,0,2:T(8,128)(2,1)} %bitcast.151), calls=%async_computation.4 | async-start | bytes 1572864 | tf_op jit(solution)/shard_map/all_to_all | solution.py:130
  187.2 10.9 %all-to-all-done.3 = bf16[1,128,48,64]{1,3,0,2:T(8,128)(2,1)S(1)} async-done(((bf16[1,128,48,64]{1,3,0,2:T(8,128)(2,1)}), bf16[1,128,48,64]{1,3,0,2:T(8,128)(2,1)S(1)}, u32[]{:S(2)}, u32[]{:S(2)}) %all-to-all-start.3) | async-done | bytes 786464 | tf_op jit(solution)/shard_map/all_to_all | solution.py:130
  198.1 4.7 %all-to-all-start.1 = ((bf16[1,128,48,64]{1,3,0,2:T(8,128)(2,1)}), bf16[1,128,48,64]{1,3,0,2:T(8,128)(2,1)S(1)}, u32[]{:S(2)}, u32[]{:S(2)}) async-start(bf16[1,128,48,64]{1,3,0,2:T(8,128)(2,1)} %multiply_convert_fusion.1), calls=%async_computation.2 | async-start | bytes 1572864 | tf_op jit(solution)/shard_map/all_to_all | solution.py:128
  204.1 12.8 %all-to-all-done.1 = bf16[1,128,48,64]{1,3,0,2:T(8,128)(2,1)S(1)} async-done(((bf16[1,128,48,64]{1,3,0,2:T(8,128)(2,1)}), bf16[1,128,48,64]{1,3,0,2:T(8,128)(2,1)S(1)}, u32[]{:S(2)}, u32[]{:S(2)}) %all-to-all-start.1) | async-done | bytes 786464 | tf_op jit(solution)/shard_map/all_to_all | solution.py:128
  217.8 30.9 %while.10 = (s32[]{:T(128)}, bf16[4,1,512,3,64]{2,4,3,1,0:T(8,128)(2,1)}, bf16[4,1,512,3,64]{2,4,3,1,0:T(8,128)(2,1)S(1)}, bf16[1,2048,3,64]{1,3,2,0:T(8,128)(2,...) while((s32[]{:T(128)}, bf16[4,1,512,3,64]{2,4,3,1,0:T(8,128)(2,1)}, ...), condition=%wide.region_8.9_spmd, body=%wide.region_5.8_spmd.sunk | while | flops 830667264 | bytes 42904164 | solution.py:108
  217.8 1.9 bitcast_reduce_fusion.2
  219.8 2.5 fusion.38
  222.3 3.3 %fusion.39 = bf16[4,1,512,3,64]{2,4,3,1,0:T(8,128)(2,1)} fusion(bf16[4,1,512,3,64]{2,4,3,1,0:T(8,128)(2,1)} %get-tuple-element.102, s32[]{:T(128)} %get-tuple-element.101, f32[3,512,2048]{2,1,0:T(8,128)S(1)} %get-tuple-element.93, f32[512,3]{0,1:T(4,128)S(1)} %broadcast_maximum_fusion.2, bf16[1,2048,3,64]{1,3,2,0:T(8,128)(2,1)S(1)} %copy-done.4, ...), kind=kOutput, calls=%fused_computation.11.clone.1 | convolution fusion | flops 412286976 | bytes 13578752 | tf_op jit(solution)/shard_map/while/body/eval_jaxpr/iths,ishd->ithd/dot_general | solution.py:85
  225.6 1.9 bitcast_reduce_fusion.2
  227.5 2.5 fusion.38
  230.0 3.3 %fusion.39 = bf16[4,1,512,3,64]{2,4,3,1,0:T(8,128)(2,1)} fusion(bf16[4,1,512,3,64]{2,4,3,1,0:T(8,128)(2,1)} %get-tuple-element.102, s32[]{:T(128)} %get-tuple-element.101, f32[3,512,2048]{2,1,0:T(8,128)S(1)} %get-tuple-element.93, f32[512,3]{0,1:T(4,128)S(1)} %broadcast_maximum_fusion.2, bf16[1,2048,3,64]{1,3,2,0:T(8,128)(2,1)S(1)} %copy-done.4, ...), kind=kOutput, calls=%fused_computation.11.clone.1 | convolution fusion | flops 412286976 | bytes 13578752 | tf_op jit(solution)/shard_map/while/body/eval_jaxpr/iths,ishd->ithd/dot_general | solution.py:85
  233.3 1.9 bitcast_reduce_fusion.2
  235.2 2.5 fusion.38
  237.7 3.3 %fusion.39 = bf16[4,1,512,3,64]{2,4,3,1,0:T(8,128)(2,1)} fusion(bf16[4,1,512,3,64]{2,4,3,1,0:T(8,128)(2,1)} %get-tuple-element.102, s32[]{:T(128)} %get-tuple-element.101, f32[3,512,2048]{2,1,0:T(8,128)S(1)} %get-tuple-element.93, f32[512,3]{0,1:T(4,128)S(1)} %broadcast_maximum_fusion.2, bf16[1,2048,3,64]{1,3,2,0:T(8,128)(2,1)S(1)} %copy-done.4, ...), kind=kOutput, calls=%fused_computation.11.clone.1 | convolution fusion | flops 412286976 | bytes 13578752 | tf_op jit(solution)/shard_map/while/body/eval_jaxpr/iths,ishd->ithd/dot_general | solution.py:85
  243.0 2.5 fusion.38
  245.4 3.3 %fusion.39 = bf16[4,1,512,3,64]{2,4,3,1,0:T(8,128)(2,1)} fusion(bf16[4,1,512,3,64]{2,4,3,1,0:T(8,128)(2,1)} %get-tuple-element.102, s32[]{:T(128)} %get-tuple-element.101, f32[3,512,2048]{2,1,0:T(8,128)S(1)} %get-tuple-element.93, f32[512,3]{0,1:T(4,128)S(1)} %broadcast_maximum_fusion.2, bf16[1,2048,3,64]{1,3,2,0:T(8,128)(2,1)S(1)} %copy-done.4, ...), kind=kOutput, calls=%fused_computation.11.clone.1 | convolution fusion | flops 412286976 | bytes 13578752 | tf_op jit(solution)/shard_map/while/body/eval_jaxpr/iths,ishd->ithd/dot_general | solution.py:85
  250.9 5.2 %all_to_all.81 = bf16[8,2,1,128,3,64]{3,0,5,4,2,1:T(8,128)(2,1)S(1)} all-to-all(bf16[8,2,1,128,3,64]{3,0,5,4,2,1:T(8,128)(2,1)S(1)} %copy.39), channel_id=1, replica_groups=mesh['seq_0'=4,'seq_1'=2,'seq_2'=2,'fsdp'=8] {'seq_2'}, dimensions={1} | all-to-all | bytes 1572864 | tf_op jit(solution)/shard_map/all_to_all | solution.py:33
  257.0 16.5 %all_to_all.82 = bf16[8,2,1,128,3,64]{3,1,5,4,2,0:T(2,128)(2,1)S(1)} all-to-all(bf16[8,2,1,128,3,64]{3,1,5,4,2,0:T(2,128)(2,1)S(1)} %copy.40), channel_id=1, replica_groups=mesh['seq_0'=4,'seq_1'=2,'seq_2'=2,'fsdp'=8] {'seq_0','seq_1'}, dimensions={0} | all-to-all | bytes 1572864 | tf_op jit(solution)/shard_map/all_to_all | solution.py:33
  (58 shorter events, 20.4 us)
Async XLA Ops:
  6.5 19.6 %copy-start.7 = (f32[3,24]{1,0:T(4,128)S(1)}, f32[3,24]{1,0:T(4,128)}, u32[]{:S(2)}) copy-start(f32[3,24]{1,0:T(4,128)} %param.11) | copy-start | bytes 868
  6.5 162.8 %reduce-scatter.2.cloned.1.call-start = ((), (), s32[]{:S(2)}) async-start(), calls=%async_computation.7 | async-start | bytes 14155776 | tf_op jit(solution)/shard_map/reduce_scatter | solution.py:119
  26.1 2.3 copy-start.1
  35.5 1.1 copy-start.2
  35.6 1.6 copy-start.5
  37.1 11.6 %copy-start.6 = (f32[3072]{0:T(1024)S(1)}, f32[3072]{0:T(1024)}, u32[]{:S(2)}) copy-start(f32[3072]{0:T(1024)} %param.14) | copy-start | bytes 36868
  37.1 11.6 %copy-start.3 = (bf16[1,128,3072]{2,1,0:T(8,128)(2,1)S(1)}, bf16[1,128,3072]{2,1,0:T(8,128)(2,1)}, u32[]{:S(2)}) copy-start(bf16[1,128,3072]{2,1,0:T(8,128)(2,1)} %param.13) | copy-start | bytes 2359300
  39.1 141.1 %all-to-all-start.2 = ((bf16[1,128,48,64]{1,3,0,2:T(8,128)(2,1)}), bf16[1,128,48,64]{1,3,0,2:T(8,128)(2,1)S(1)}, u32[]{:S(2)}, u32[]{:S(2)}) async-start(bf16[1,128,48,64]{1,3,0,2:T(8,128)(2,1)} %fusion.30), calls=%async_computation.3 | async-start | bytes 1572864 | tf_op jit(solution)/shard_map/all_to_all | solution.py:129
  169.3 16.5 %copy-start = (f32[128,3072]{0,1:T(8,128)S(1)}, f32[128,3072]{0,1:T(8,128)}, u32[]{:S(2)}) copy-start(f32[128,3072]{0,1:T(8,128)} %reduce-scatter.2.cloned.1.call-done) | copy-start | bytes 4718596
  180.2 17.9 %all-to-all-start.3 = ((bf16[1,128,48,64]{1,3,0,2:T(8,128)(2,1)}), bf16[1,128,48,64]{1,3,0,2:T(8,128)(2,1)S(1)}, u32[]{:S(2)}, u32[]{:S(2)}) async-start(bf16[1,128,48,64]{1,3,0,2:T(8,128)(2,1)} %bitcast.151), calls=%async_computation.4 | async-start | bytes 1572864 | tf_op jit(solution)/shard_map/all_to_all | solution.py:130
  198.1 18.7 %all-to-all-start.1 = ((bf16[1,128,48,64]{1,3,0,2:T(8,128)(2,1)}), bf16[1,128,48,64]{1,3,0,2:T(8,128)(2,1)S(1)}, u32[]{:S(2)}, u32[]{:S(2)}) async-start(bf16[1,128,48,64]{1,3,0,2:T(8,128)(2,1)} %multiply_convert_fusion.1), calls=%async_computation.2 | async-start | bytes 1572864 | tf_op jit(solution)/shard_map/all_to_all | solution.py:128
  219.8 2.5 copy-start.4
  227.5 2.5 copy-start.4
  235.2 2.5 copy-start.4
  242.9 2.5 copy-start.4
Sparse Core Ops, SparseCore 0:
  35.7 133.5 reduce-scatter.1
where the time goes:
time: 282 us
  waiting for transfers between devices  152 us (54%)
  blocking collectives  39.5 us (14%)
  matrix products  28 us (10%)
  starting transfers between devices  18 us (6%)
  other arithmetic  16.6 us (6%)
  local copies, waits for them, and re-layouts  13.6 us (5%)
  between operations  13.6 us (5%)
    reduce_scatter x1, waiting for transfers between devices, per_device(): lax.psum_scatter(jnp.dot(group_rows, local_weight, preferred_element_type...  119 us
    all_to_all x2, blocking collectives, exchange_in_order(): whole = lax.all_to_all(whole, axes[k], k, k, tiled=True)  21.8 us
    all_to_all x1, blocking collectives, per_device(): lax.all_to_all(flat_rows, 'fsdp', split_axis=1, concat_axis=0, tiled=True)  17.7 us
    dot_general x4, matrix products, attend_block(): jnp.einsum('iths,ishd->ithd', probability.astype(jnp.bfloat16), value_vie...  13.2 us
    all_to_all x1, waiting for transfers between devices, per_device(): lax.all_to_all(query_view, SEQ, split_axis=2, concat_axis=1, tiled=True)  12.8 us
    all_to_all x1, waiting for transfers between devices, per_device(): lax.all_to_all(value_view, SEQ, split_axis=2, concat_axis=1, tiled=True)  10.9 us
    reduce_sum x4, other arithmetic, attend_block(): running_sum = jnp.sum(probability, axis=-1)  9.85 us
    all_to_all x1, starting transfers between devices, per_device(): lax.all_to_all(key_norm, SEQ, split_axis=2, concat_axis=1, tiled=True)  9.47 us
  transfers between devices with their start and end apart: 4, of which 4 were waited for; matrix products, arithmetic and copies ran while one was open for 3% of the time, Pallas kernels for 0%

commit v1 on v0

v1 whole, which is shorter than its diff:
```python
import math

import jax
import jax.numpy as jnp
from jax import lax
from jax.experimental import pallas as pl
from jax.experimental.pallas import tpu as pltpu
from jax.sharding import Mesh
from jax.sharding import PartitionSpec as P

HEADS = 48
HDIM = 64
BLOCK = 128
NORM_FLOOR = 0.25
EXP2_SCALE = HDIM**-0.5 * math.log2(math.e)
QUERY_BLOCK = 256
KEY_CHUNK = 128
LANES = 128
COLUMN_BLOCK = 256
SEQ = ("z", "yh", "co")
FSDP = ("yl", "x")
Z, X = 4, 4


def head_norm(projected, gain_row):
    shaped = projected.reshape(projected.shape[:-1] + (-1, HDIM))
    average = jnp.mean(shaped, axis=-1, keepdims=True)
    centred = shaped - average
    spread = jnp.mean(centred * centred, axis=-1, keepdims=True)
    normed = centred * lax.rsqrt(spread + NORM_FLOOR) * gain_row.reshape(-1, HDIM)
    return normed.astype(jnp.bfloat16).reshape(projected.shape)


def dequantize(weight_codes, block_scales):
    row_count, column_count = weight_codes.shape
    blocked = weight_codes.astype(jnp.float32).reshape(
        row_count // BLOCK, BLOCK, column_count // BLOCK, BLOCK
    )
    return (
        (blocked * block_scales[:, None, :, None])
        .reshape(row_count, column_count)
        .astype(jnp.bfloat16)
    )


def shift(value, axis, by, size):
    return lax.ppermute(value, axis, [(i, (i + by) % size) for i in range(size)])


def project_and_attend(tokens, weights, pairs, gain):
    token_counts = [t.shape[0] for t in tokens]
    key_counts = [p.shape[1] for p in pairs]
    total, keys = sum(token_counts), sum(key_counts)
    features, columns = tokens[0].shape[1], weights[0].shape[1]
    heads = COLUMN_BLOCK // HDIM
    blocks = total // QUERY_BLOCK
    units = heads * blocks
    nt, nw, nk = len(tokens), len(weights), len(pairs)

    def body(*refs):
        token_refs, refs = refs[:nt], refs[nt:]
        weight_refs, refs = refs[:nw], refs[nw:]
        key_refs, refs = refs[:nk], refs[nk:]
        value_refs, refs = refs[:nk], refs[nk:]
        gain_ref, refs = refs[0], refs[1:]
        out_refs, refs = refs[:nt], refs[nt:]
        query_ref, value_t, score_ref, prob_ref, out_t, max_ref = refs

        at = 0
        for t, token_ref in enumerate(token_refs):
            count = token_counts[t]
            acc, row = None, 0
            for weight_ref in weight_refs:
                rows = weight_ref.shape[0]
                part = jnp.dot(
                    token_ref[:, row : row + rows],
                    weight_ref[...],
                    preferred_element_type=jnp.float32,
                )
                acc = part if acc is None else acc + part
                row += rows
            turned = acc.T.reshape(heads, HDIM, count)
            centred = turned - jnp.mean(turned, axis=1, keepdims=True)
            spread = jnp.mean(centred * centred, axis=1, keepdims=True)
            gains = gain_ref[...].reshape(heads, HDIM, 1)
            normed = (centred * lax.rsqrt(spread + NORM_FLOOR) * gains).astype(jnp.bfloat16)
            nothing = jnp.zeros((HDIM, count), jnp.bfloat16)
            for h in range(heads):
                low, high = (normed[h], nothing) if h % 2 == 0 else (nothing, normed[h])
                query_ref[h, 0:HDIM, at : at + count] = low
                query_ref[h, HDIM : 2 * HDIM, at : at + count] = high
            at += count
        at = 0
        for value_ref in value_refs:
            count = value_ref.shape[0]
            value_t[:, at : at + count] = value_ref[...].T
            at += count

        def scores(unit, slot):
            h, b = unit // blocks, unit % blocks
            query = query_ref[h, :, pl.ds(pl.multiple_of(b * QUERY_BLOCK, QUERY_BLOCK), QUERY_BLOCK)]
            lanes = pl.ds(pl.multiple_of((h // 2) * LANES, LANES), LANES)
            at, top = 0, None
            for key_ref in key_refs:
                for c in range(key_ref.shape[0] // KEY_CHUNK):
                    score = jnp.dot(
                        key_ref[c * KEY_CHUNK : (c + 1) * KEY_CHUNK, lanes],
                        query,
                        preferred_element_type=jnp.float32,
                    )
                    score_ref[slot, at : at + KEY_CHUNK, :] = score
                    best = jnp.max(score.reshape(KEY_CHUNK // 8, 8, QUERY_BLOCK), axis=0)
                    top = best if top is None else jnp.maximum(top, best)
                    at += KEY_CHUNK
            max_ref[slot] = top

        def finish(unit, slot):
            h, b = unit // blocks, unit % blocks
            top = jnp.max(max_ref[slot], axis=0, keepdims=True)
            total_sum = None
            for c in range(keys // KEY_CHUNK):
                at = c * KEY_CHUNK
                prob = jnp.exp2((score_ref[slot, at : at + KEY_CHUNK, :] - top) * EXP2_SCALE)
                part = jnp.sum(prob.reshape(KEY_CHUNK // 8, 8, QUERY_BLOCK), axis=0)
                total_sum = part if total_sum is None else total_sum + part
                prob_ref[at : at + KEY_CHUNK, :] = prob.astype(jnp.bfloat16)
            rows = pl.ds(pl.multiple_of(h * HDIM, HDIM), HDIM)
            blended = jnp.dot(value_t[rows, :], prob_ref[...], preferred_element_type=jnp.float32)
            norm = jnp.sum(total_sum, axis=0, keepdims=True)
            out_t[rows, pl.ds(pl.multiple_of(b * QUERY_BLOCK, QUERY_BLOCK), QUERY_BLOCK)] = (
                blended / norm
            )

        scores(0, 0)

        def step(unit, carry):
            slot = unit % 2
            scores(jnp.minimum(unit + 1, units - 1), 1 - slot)
            finish(unit, slot)
            return carry

        lax.fori_loop(0, units, step, 0)
        at = 0
        for t, out_ref in enumerate(out_refs):
            out_ref[...] = out_t[:, at : at + token_counts[t]].T.astype(jnp.bfloat16)
            at += token_counts[t]

    def half(count, which):
        return pl.BlockSpec((None, count, COLUMN_BLOCK), lambda i: (which, 0, i))

    return pl.pallas_call(
        body,
        grid=(columns // COLUMN_BLOCK,),
        in_specs=[pl.BlockSpec((t, features), lambda i: (0, 0)) for t in token_counts]
        + [pl.BlockSpec((w.shape[0], COLUMN_BLOCK), lambda i: (0, i)) for w in weights]
        + [half(n, 0) for n in key_counts]
        + [half(n, 1) for n in key_counts]
        + [pl.BlockSpec((COLUMN_BLOCK, 1), lambda i: (i, 0))],
        out_specs=[pl.BlockSpec((t, COLUMN_BLOCK), lambda i: (0, i)) for t in token_counts],
        out_shape=[jax.ShapeDtypeStruct((t, columns), jnp.bfloat16) for t in token_counts],
        scratch_shapes=[
            pltpu.VMEM((heads, 2 * HDIM, total), jnp.bfloat16),
            pltpu.VMEM((COLUMN_BLOCK, keys), jnp.bfloat16),
            pltpu.VMEM((2, keys, QUERY_BLOCK), jnp.float32),
            pltpu.VMEM((keys, QUERY_BLOCK), jnp.bfloat16),
            pltpu.VMEM((COLUMN_BLOCK, total), jnp.float32),
            pltpu.VMEM((2, 8, QUERY_BLOCK), jnp.float32),
        ],
        compiler_params=pltpu.CompilerParams(
            dimension_semantics=("arbitrary",), vmem_limit_bytes=56 << 20
        ),
    )(*tokens, *weights, *pairs, *pairs, gain)


def per_device(patches, weight_codes, block_scales, key_proj, value_proj, query_gain, key_gain):
    tokens, features = patches.shape[1:]
    rows = weight_codes.shape[0]
    share = features // Z
    z, co, yl, x = (lax.axis_index(a) for a in ("z", "co", "yl", "x"))

    both = jnp.stack([head_norm(key_proj[0].astype(jnp.float32), key_gain), value_proj[0]])

    def quarter(by):
        at = ((z + by) % Z) * share
        return lax.dynamic_slice(both, (0, 0, at), (2, tokens, share))

    near = quarter(0)
    far = jnp.concatenate([shift(quarter(by), "z", by, Z) for by in (1, 3, 2)], axis=1)
    pairs = [near, far, shift(near, "yh", 1, 2), shift(far, "yh", 1, 2)]
    pairs = pairs + [shift(p, "co", 1, 2) for p in pairs]

    own = dequantize(
        lax.dynamic_slice(weight_codes, (0, z * share), (rows, share)),
        lax.dynamic_slice(
            block_scales, (0, z * (share // BLOCK)), (rows // BLOCK, share // BLOCK)
        ),
    )
    y_moves = []
    for y in range(4):
        for core, by in ((0, 1), (1, 3)):
            to = (y + by) % 4
            y_moves.append((((y // 2) * 2 + core) * 2 + y % 2, ((to // 2) * 2 + core) * 2 + to % 2))
    half = rows // 2
    mine = lax.ppermute(
        lax.dynamic_slice(own, (co * half, 0), (half, share)), ("yh", "co", "yl"), y_moves
    )
    theirs = shift(mine, "co", 1, 2)
    unit = jnp.concatenate(
        [own, jnp.where(co == 0, mine, theirs), jnp.where(co == 0, theirs, mine)]
    )
    x_moves = [(core * X + i, core * X + (i + by) % X) for core, by in ((0, 1), (1, 3)) for i in range(X)]
    mine_near = lax.ppermute(unit, ("co", "x"), x_moves)
    mine_far = shift(lax.dynamic_slice(unit, (co * rows, 0), (rows, share)), "x", 2, X)
    weights = [unit, mine_near, mine_far, shift(mine_near, "co", 1, 2), shift(mine_far, "co", 1, 2)]

    back = jnp.where(co == 0, 3, 1)
    order = [
        (yl, x),
        (1 - yl, x),
        (yl, x + back),
        (1 - yl, x + back),
        ((yl + co) % 2, x + 2),
        (yl, x + 4 - back),
        (1 - yl, x + 4 - back),
        ((yl + 1 - co) % 2, x + 2),
    ]
    ordered = jnp.concatenate(
        [
            lax.dynamic_slice(patches[0], (0, (a * X + b % X) * rows), (tokens, rows))
            for a, b in order
        ],
        axis=1,
    )
    steps = (0, 1, 3, 2)
    arrived = [ordered] + [shift(ordered, "z", by, Z) for by in steps[1:]]

    gain = lax.dynamic_slice(query_gain, (z * share,), (share,)).reshape(share, 1)
    done = project_and_attend(arrived, weights, pairs, gain)
    result = jnp.zeros((tokens, features), jnp.bfloat16)
    for by, piece in zip(steps, done):
        if by:
            piece = shift(piece, "z", Z - by, Z)
        result = lax.dynamic_update_slice(result, piece, (0, ((z + by) % Z) * share))
    return result[None]


def solution(mesh):
    split = Mesh(mesh.devices.reshape(Z, 2, 2, 2, X), ("z", "yh", "co", "yl", "x"))
    placed = (
        P(FSDP, SEQ, None),
        P(FSDP, None),
        P(FSDP, None),
        P(FSDP, SEQ, None),
        P(FSDP, SEQ, None),
        P(),
        P(),
    )
    return jax.shard_map(
        per_device, mesh=split, in_specs=placed, out_specs=P(FSDP, SEQ, None), check_vma=False
    )
```

time: 282 us -> 137 us (0.49)
  waiting for transfers between devices: 152 us -> 47.2 us
  blocking collectives: 39.5 us -> 0 us
  Pallas kernels: 0 us -> 32.2 us
  matrix products: 28 us -> 0 us
  between operations: 13.6 us -> 0.3 us
  other arithmetic: 16.6 us -> 6.26 us
  starting transfers between devices: 18 us -> 28 us
  local copies, waits for them, and re-layouts: 13.6 us -> 20.1 us
    reduce_scatter x1 -> x0, waiting for transfers between devices: 119 us -> none  [per_device(): lax.psum_scatter(jnp.dot(group_rows, local_weight, preferred_element_type...]
    ppermute x0 -> x21, waiting for transfers between devices: none -> 47.2 us  [the longest x19 38.1 us: shift(): lax.ppermute(value, axis, [(i, (i + by) % size) for i in range(size)])]
    all_to_all x3 -> x0, blocking collectives: 39.5 us -> none  [the longest x2 21.8 us: exchange_in_order(): whole = lax.all_to_all(whole, axes[k], k, k, tiled=True)]
    all_to_all x3 -> x0, waiting for transfers between devices: 32.8 us -> none  [the longest x1 12.8 us: per_device(): lax.all_to_all(query_view, SEQ, split_axis=2, concat_axis=1, tiled=True)]
    pallas_call x0 -> x1, Pallas kernels: none -> 32.2 us  [project_and_attend(): pl.pallas_call(body, grid=(columns // COLUMN_BLOCK,), in_specs=[pl.BlockS...]
    ppermute x0 -> x21, starting transfers between devices: none -> 28 us  [the longest x19 22.7 us: shift(): lax.ppermute(value, axis, [(i, (i + by) % size) for i in range(size)])]
    dot_general x9 -> x0, matrix products: 28 us -> none  [the longest x4 13.2 us: attend_block(): jnp.einsum('iths,ishd->ithd', probability.astype(jnp.bfloat16), value_vie...]
    all_to_all x3 -> x0, starting transfers between devices: 18 us -> none  [the longest x1 9.47 us: per_device(): lax.all_to_all(key_norm, SEQ, split_axis=2, concat_axis=1, tiled=True)]
  transfers between devices with their start and end apart: 4 -> 21, of which waited for: 4 -> 8; matrix products, arithmetic and copies ran while one was open for 3% -> 11% of each run, Pallas kernels for 0% -> 0%
where the time goes in v1:
time: 137 us; the launch traced here: 134 us
  waiting for transfers between devices  47.2 us (34%)
  Pallas kernels  32.2 us (24%)
  starting transfers between devices  28 us (20%)
  local copies, waits for them, and re-layouts  20.1 us (15%)
  other arithmetic  6.26 us (5%)
    ppermute x19, waiting for transfers between devices, shift(): lax.ppermute(value, axis, [(i, (i + by) % size) for i in range(size)])  38.1 us
    pallas_call x1, Pallas kernels, project_and_attend(): pl.pallas_call(body, grid=(columns // COLUMN_BLOCK,), in_specs=[pl.BlockS...  32.2 us
    ppermute x19, starting transfers between devices, shift(): lax.ppermute(value, axis, [(i, (i + by) % size) for i in range(size)])  22.7 us
    unnamed x41, local copies, waits for them, and re-layouts  11.1 us
    ppermute x1, waiting for transfers between devices, per_device(): lax.ppermute(lax.dynamic_slice(own, (co * half, 0), (half, share)), ('yh'...  9.14 us
    ppermute x1, starting transfers between devices, per_device(): lax.ppermute(lax.dynamic_slice(own, (co * half, 0), (half, share)), ('yh'...  2.8 us
  transfers between devices with their start and end apart: 21, of which 8 were waited for; matrix products, arithmetic and copies ran while one was open for 11% of the time, Pallas kernels for 0%

profile of v1, /device:TPU:1, one launch (start us, length us, event | category | flops | bytes accessed | tf_op | source)
XLA Modules:
  0.0 134.2 jit_solution(15916348252800574449)
XLA Ops:
  2.6 1.7 %copy.9 = f32[1,128,3072]{2,1,0:T(8,128)} copy(f32[1,128,3072]{1,2,0:T(8,128)S(1)} %bitcast.36) | data formatting | bytes 3145728 | tf_op jit(solution)/shard_map/sub | solution.py:28
  4.3 2.1 %multiply_convert_fusion = bf16[1,128,3072]{2,1,0:T(8,128)(2,1)S(1)} fusion(f32[1,128,3072]{2,1,0:T(8,128)S(1)} %copy.10, f32[1,128,3072]{2,1,0:T(8,128)} %copy.9, f32[3072]{0:T(1024)S(1)} %copy-done.15, bf16[1,128,3072]{2,1,0:T(8,128)(2,1)} %param.10), kind=kLoop, calls=%fused_computation.8 | loop fusion | flops 1966080 | bytes 4730880 | tf_op jit(solution)/shard_map/convert_element_type | solution.py:31
  7.3 2.5 %collective-permute-start.9 = (bf16[2,128,768]{2,1,0:T(8,128)(2,1)S(1)}, bf16[2,128,768]{2,1,0:T(8,128)(2,1)S(1)}, u32[]{:S(2)}, u32[]{:S(2)}) collective-permute-start(bf16[2,128,768]{2,1,0:T(8,128)(2,1)S(1)} %get-tuple-element.15), channel_id=1, source_target_pairs={{0,32},{32,64},{64,96},{96,0},{1,33},{33,65},{65,97},{97,1},{2,34}... | collective-permute-start | bytes 1179656 | tf_op jit(solution)/shard_map/ppermute | solution.py:47
  9.8 2.1 %collective-permute-start.10 = (bf16[2,128,768]{2,1,0:T(8,128)(2,1)S(1)}, bf16[2,128,768]{2,1,0:T(8,128)(2,1)S(1)}, u32[]{:S(2)}, u32[]{:S(2)}) collective-permute-start(bf16[2,128,768]{2,1,0:T(8,128)(2,1)S(1)} %get-tuple-element.16), channel_id=1, source_target_pairs={{0,96},{32,0},{64,32},{96,64},{1,97},{33,1},{65,33},{97,65},{2,98}... | collective-permute-start | bytes 1179656 | tf_op jit(solution)/shard_map/ppermute | solution.py:47
  13.5 1.6 %fusion = bf16[384,768]{1,0:T(8,128)(2,1)S(1)} fusion(f32[48,8,6,128]{3,2,1,0:T(8,128)S(1)} %bitcast.37, s32[384,3072]{1,0:T(8,128)} %param.8, s32[]{:T(128)S(6)} %select_n.143), kind=kLoop, calls=%fused_computation.11 | loop fusion | flops 884736 | bytes 2949124 | tf_op jit(solution)/shard_map/convert_element_type | solution.py:42
  16.0 2.8 %collective-permute-start.3 = (bf16[192,768]{1,0:T(8,128)(2,1)S(1)}, bf16[192,768]{1,0:T(8,128)(2,1)}, u32[]{:S(2)}, u32[]{:S(2)}) collective-permute-start(bf16[192,768]{1,0:T(8,128)(2,1)S(1)} %constant_dynamic-slice_fusion.1), channel_id=1, source_target_pairs={{0,4},{8,28},{4,16},{12,8},{16,20},{24,12},{20,0},{28,24},{1,5},{9... | collective-permute-start | bytes 884744 | tf_op jit(solution)/shard_map/ppermute | solution.py:204
  21.7 9.1 %collective-permute-done.3 = bf16[192,768]{1,0:T(8,128)(2,1)} collective-permute-done((bf16[192,768]{1,0:T(8,128)(2,1)S(1)}, bf16[192,768]{1,0:T(8,128)(2,1)}, u32[]{:S(2)}, u32[]{:S(2)}) %collective-permute-start.3) | collective-permute-done | bytes 294944 | tf_op jit(solution)/shard_map/ppermute | solution.py:204
  31.5 1.6 %collective-permute-start.13 = (bf16[2,384,768]{2,1,0:T(8,128)(2,1)S(1)}, bf16[2,384,768]{2,1,0:T(8,128)(2,1)S(1)}, u32[]{:S(2)}, u32[]{:S(2)}) collective-permute-start(bf16[2,384,768]{2,1,0:T(8,128)(2,1)S(1)} %constant_dynamic-update-slice_fusion.refs_10_.refs_18_), channel_id=1, source_target_pairs={{0,16},{16,0},{1,17},{17,1},{2,18},{18,2},{3,19},{19,3},{4,20},{20... | collective-permute-start | bytes 3538952 | tf_op jit(solution)/shard_map/ppermute | solution.py:47
  34.4 2.5 %collective-permute-start.5 = (bf16[768,768]{1,0:T(8,128)(2,1)S(1)}, bf16[768,768]{1,0:T(8,128)(2,1)}, u32[]{:S(2)}, u32[]{:S(2)}) collective-permute-start(bf16[768,768]{1,0:T(8,128)(2,1)S(1)} %pad_maximum_fusion.refs_4_), channel_id=1, source_target_pairs={{0,1},{1,2},{2,3},{3,0},{8,11},{9,8},{10,9},{11,10},{4,5},{5,6},{6... | collective-permute-start | bytes 3538952 | tf_op jit(solution)/shard_map/ppermute | solution.py:212
  36.9 1.5 %bitcast_dynamic-update-slice_fusion.7 = bf16[128,3072]{1,0:T(8,128)(2,1)} fusion(bf16[128,3072]{1,0:T(8,128)(2,1)} %bitcast_dynamic-update-slice_fusion.8, bf16[1,128,3072]{2,1,0:T(8,128)(2,1)} %param.7, s32[]{:T(128)S(6)} %select_n.137), kind=kLoop, calls=%fused_computation.26 | loop fusion | bytes 196612
  38.4 1.5 %bitcast_dynamic-update-slice_fusion.6 = bf16[128,3072]{1,0:T(8,128)(2,1)} fusion(bf16[128,3072]{1,0:T(8,128)(2,1)} %bitcast_dynamic-update-slice_fusion.7, bf16[1,128,3072]{2,1,0:T(8,128)(2,1)} %param.7, s32[]{:T(128)S(6)} %select_n.139), kind=kLoop, calls=%fused_computation.25 | loop fusion | bytes 196612
  40.0 1.5 %bitcast_dynamic-update-slice_fusion.5 = bf16[128,3072]{1,0:T(8,128)(2,1)} fusion(bf16[128,3072]{1,0:T(8,128)(2,1)} %bitcast_dynamic-update-slice_fusion.6, bf16[1,128,3072]{2,1,0:T(8,128)(2,1)} %param.7, s32[]{:T(128)S(6)} %select_n.140), kind=kLoop, calls=%fused_computation.24 | loop fusion | bytes 196612
  41.5 1.5 %bitcast_dynamic-update-slice_fusion.4.refs_0_ = bf16[128,3072]{1,0:T(8,128)(2,1)} fusion(bf16[128,3072]{1,0:T(8,128)(2,1)} %bitcast_dynamic-update-slice_fusion.5, bf16[1,128,3072]{2,1,0:T(8,128)(2,1)} %param.7, s32[]{:T(128)S(6)} %select_n.142), kind=kLoop, calls=%fused_computation.23 | loop fusion | bytes 196612 | tf_op jit(solution)/shard_map/concatenate | solution.py:227
  44.9 1.8 %collective-permute-start.1 = (bf16[128,3072]{1,0:T(8,128)(2,1)}, bf16[128,3072]{1,0:T(8,128)(2,1)}, u32[]{:S(2)}, u32[]{:S(2)}) collective-permute-start(bf16[128,3072]{1,0:T(8,128)(2,1)} %bitcast_dynamic-update-slice_fusion.4.refs_0_), channel_id=1, source_target_pairs={{0,96},{32,0},{64,32},{96,64},{1,97},{33,1},{65,33},{97,65},{2,98}... | collective-permute-start | bytes 2359304 | tf_op jit(solution)/shard_map/ppermute | solution.py:47
  47.2 16.8 %collective-permute-done.refs_1_ = bf16[128,3072]{1,0:T(8,128)(2,1)} collective-permute-done((bf16[128,3072]{1,0:T(8,128)(2,1)}, bf16[128,3072]{1,0:T(8,128)(2,1)}, u32[]{:S(2)}, u32[]{:S(2)}) %collective-permute-start) | collective-permute-done | bytes 786464 | tf_op jit(solution)/shard_map/ppermute | solution.py:47
  64.0 1.9 %collective-permute-start.17 = (bf16[2,384,768]{2,1,0:T(8,128)(2,1)S(1)}, bf16[2,384,768]{2,1,0:T(8,128)(2,1)S(1)}, u32[]{:S(2)}, u32[]{:S(2)}) collective-permute-start(bf16[2,384,768]{2,1,0:T(8,128)(2,1)S(1)} %collective-permute-done.13.refs_12_.refs_20_), channel_id=1, source_target_pairs={{0,8},{8,0},{1,9},{9,1},{2,10},{10,2},{3,11},{11,3},{4,12},{12,4},... | collective-permute-start | bytes 3538952 | tf_op jit(solution)/shard_map/ppermute | solution.py:47
  66.0 2.4 %collective-permute-start.2 = (bf16[128,3072]{1,0:T(8,128)(2,1)}, bf16[128,3072]{1,0:T(8,128)(2,1)S(1)}, u32[]{:S(2)}, u32[]{:S(2)}) collective-permute-start(bf16[128,3072]{1,0:T(8,128)(2,1)} %bitcast_dynamic-update-slice_fusion.4.refs_0_), channel_id=1, source_target_pairs={{0,64},{32,96},{64,0},{96,32},{1,65},{33,97},{65,1},{97,33},{2,66}... | collective-permute-start | bytes 2359304 | tf_op jit(solution)/shard_map/ppermute | solution.py:47
  68.5 10.9 %collective-permute-done.6.refs_6_ = bf16[384,768]{1,0:T(8,128)(2,1)S(1)} collective-permute-done((bf16[384,768]{1,0:T(8,128)(2,1)S(1)}, bf16[384,768]{1,0:T(8,128)(2,1)S(1)}, u32[]{:S(2)}, u32[]{:S(2)}) %collective-permute-start.6) | collective-permute-done | bytes 589856 | tf_op jit(solution)/shard_map/ppermute | solution.py:47
  79.3 1.9 %collective-permute-start.8 = (bf16[384,768]{1,0:T(8,128)(2,1)S(1)}, bf16[384,768]{1,0:T(8,128)(2,1)S(1)}, u32[]{:S(2)}, u32[]{:S(2)}) collective-permute-start(bf16[384,768]{1,0:T(8,128)(2,1)S(1)} %collective-permute-done.6.refs_6_), channel_id=1, source_target_pairs={{0,8},{8,0},{1,9},{9,1},{2,10},{10,2},{3,11},{11,3},{4,12},{12,4},... | collective-permute-start | bytes 1769480 | tf_op jit(solution)/shard_map/ppermute | solution.py:47
  83.0 3.5 %collective-permute-done.2.refs_3_ = bf16[128,3072]{1,0:T(8,128)(2,1)S(1)} collective-permute-done((bf16[128,3072]{1,0:T(8,128)(2,1)}, bf16[128,3072]{1,0:T(8,128)(2,1)S(1)}, u32[]{:S(2)}, u32[]{:S(2)}) %collective-permute-start.2) | collective-permute-done | bytes 786464 | tf_op jit(solution)/shard_map/ppermute | solution.py:47
  89.4 32.2 %shard_map.73 = (bf16[128,768]{1,0:T(8,128)(2,1)}, bf16[128,768]{1,0:T(8,128)(2,1)}, bf16[128,768]{1,0:T(8,128)(2,1)}, bf16[128,768]{1,0:T(8,128)(2,1)}) custom-call(bf16[128,3072]{1,0:T(8,128)(2,1)} %bitcast_dynamic-update-slice_fusion.4.refs_0_, bf16[128,3072]{1,0:T(8,128)(2,1)} %collective-permute-done.refs_1_, ...), custom_call_target="tpu_custom_call" | custom-call | tf_op jit(solution)/shard_map/pallas_call | solution.py:151
  123.2 2.4 %collective-permute-start.20 = (bf16[128,768]{1,0:T(8,128)(2,1)}, bf16[128,768]{1,0:T(8,128)(2,1)S(1)}, u32[]{:S(2)}, u32[]{:S(2)}) collective-permute-start(bf16[128,768]{1,0:T(8,128)(2,1)} %get-tuple-element.12), channel_id=1, source_target_pairs={{0,64},{32,96},{64,0},{96,32},{1,65},{33,97},{65,1},{97,33},{2,66}... | collective-permute-start | bytes 589832 | tf_op jit(solution)/shard_map/ppermute | solution.py:47
  127.2 1.7 %collective-permute-done.19 = bf16[128,768]{1,0:T(8,128)(2,1)S(1)} collective-permute-done((bf16[128,768]{1,0:T(8,128)(2,1)}, bf16[128,768]{1,0:T(8,128)(2,1)S(1)}, u32[]{:S(2)}, u32[]{:S(2)}) %collective-permute-start.19) | collective-permute-done | bytes 196640 | tf_op jit(solution)/shard_map/ppermute | solution.py:47
  128.9 4.6 %collective-permute-done.20 = bf16[128,768]{1,0:T(8,128)(2,1)S(1)} collective-permute-done((bf16[128,768]{1,0:T(8,128)(2,1)}, bf16[128,768]{1,0:T(8,128)(2,1)S(1)}, u32[]{:S(2)}, u32[]{:S(2)}) %collective-permute-start.20) | collective-permute-done | bytes 196640 | tf_op jit(solution)/shard_map/ppermute | solution.py:47
  (87 shorter events, 21.6 us)
Async XLA Ops:
  7.3 23.5 %collective-permute-start.9 = (bf16[2,128,768]{2,1,0:T(8,128)(2,1)S(1)}, bf16[2,128,768]{2,1,0:T(8,128)(2,1)S(1)}, u32[]{:S(2)}, u32[]{:S(2)}) collective-permute-start(bf16[2,128,768]{2,1,0:T(8,128)(2,1)S(1)} %get-tuple-element.15), channel_id=1, source_target_pairs={{0,32},{32,64},{64,96},{96,0},{1,33},{33,65},{65,97},{97,1},{2,34}... | collective-permute-start | bytes 1179656 | tf_op jit(solution)/shard_map/ppermute | solution.py:47
  9.8 21.6 %collective-permute-start.10 = (bf16[2,128,768]{2,1,0:T(8,128)(2,1)S(1)}, bf16[2,128,768]{2,1,0:T(8,128)(2,1)S(1)}, u32[]{:S(2)}, u32[]{:S(2)}) collective-permute-start(bf16[2,128,768]{2,1,0:T(8,128)(2,1)S(1)} %get-tuple-element.16), channel_id=1, source_target_pairs={{0,96},{32,0},{64,32},{96,64},{1,97},{33,1},{65,33},{97,65},{2,98}... | collective-permute-start | bytes 1179656 | tf_op jit(solution)/shard_map/ppermute | solution.py:47
  11.9 19.6 %collective-permute-start.11 = (bf16[2,128,768]{2,1,0:T(8,128)(2,1)S(1)}, bf16[2,128,768]{2,1,0:T(8,128)(2,1)S(1)}, u32[]{:S(2)}, u32[]{:S(2)}) collective-permute-start(bf16[2,128,768]{2,1,0:T(8,128)(2,1)S(1)} %get-tuple-element.13), channel_id=1, source_target_pairs={{0,64},{32,96},{64,0},{96,32},{1,65},{33,97},{65,1},{97,33},{2,66}... | collective-permute-start | bytes 1179656 | tf_op jit(solution)/shard_map/ppermute | solution.py:47
  16.0 14.9 %collective-permute-start.3 = (bf16[192,768]{1,0:T(8,128)(2,1)S(1)}, bf16[192,768]{1,0:T(8,128)(2,1)}, u32[]{:S(2)}, u32[]{:S(2)}) collective-permute-start(bf16[192,768]{1,0:T(8,128)(2,1)S(1)} %constant_dynamic-slice_fusion.1), channel_id=1, source_target_pairs={{0,4},{8,28},{4,16},{12,8},{16,20},{24,12},{20,0},{28,24},{1,5},{9... | collective-permute-start | bytes 884744 | tf_op jit(solution)/shard_map/ppermute | solution.py:204
  18.8 25.1 %collective-permute-start.12 = (bf16[2,128,768]{2,1,0:T(8,128)(2,1)}, bf16[2,128,768]{2,1,0:T(8,128)(2,1)}, u32[]{:S(2)}, u32[]{:S(2)}) collective-permute-start(bf16[2,128,768]{2,1,0:T(8,128)(2,1)} %get-tuple-element.14.refs_9_.refs_17_), channel_id=1, source_target_pairs={{0,16},{16,0},{1,17},{17,1},{2,18},{18,2},{3,19},{19,3},{4,20},{20... | collective-permute-start | bytes 1179656 | tf_op jit(solution)/shard_map/ppermute | solution.py:47
  30.9 14.1 %collective-permute-start.14 = (bf16[2,128,768]{2,1,0:T(8,128)(2,1)}, bf16[2,128,768]{2,1,0:T(8,128)(2,1)}, u32[]{:S(2)}, u32[]{:S(2)}) collective-permute-start(bf16[2,128,768]{2,1,0:T(8,128)(2,1)} %get-tuple-element.14.refs_9_.refs_17_), channel_id=1, source_target_pairs={{0,8},{8,0},{1,9},{9,1},{2,10},{10,2},{3,11},{11,3},{4,12},{12,4},... | collective-permute-start | bytes 1179656 | tf_op jit(solution)/shard_map/ppermute | solution.py:47
  30.9 2.3 %collective-permute-start.4 = (bf16[192,768]{1,0:T(8,128)(2,1)}, bf16[192,768]{1,0:T(8,128)(2,1)S(1)}, u32[]{:S(2)}, u32[]{:S(2)}) collective-permute-start(bf16[192,768]{1,0:T(8,128)(2,1)} %collective-permute-done.3), channel_id=1, source_target_pairs={{0,8},{8,0},{1,9},{9,1},{2,10},{10,2},{3,11},{11,3},{4,12},{12,4},... | collective-permute-start | bytes 884744 | tf_op jit(solution)/shard_map/ppermute | solution.py:47
  31.5 15.3 %copy-start.2 = (bf16[2,384,768]{2,1,0:T(8,128)(2,1)}, bf16[2,384,768]{2,1,0:T(8,128)(2,1)S(1)}, u32[]{:S(2)}) copy-start(bf16[2,384,768]{2,1,0:T(8,128)(2,1)S(1)} %constant_dynamic-update-slice_fusion.refs_10_.refs_18_) | copy-start | bytes 3538948
  31.5 32.5 %collective-permute-start.13 = (bf16[2,384,768]{2,1,0:T(8,128)(2,1)S(1)}, bf16[2,384,768]{2,1,0:T(8,128)(2,1)S(1)}, u32[]{:S(2)}, u32[]{:S(2)}) collective-permute-start(bf16[2,384,768]{2,1,0:T(8,128)(2,1)S(1)} %constant_dynamic-update-slice_fusion.refs_10_.refs_18_), channel_id=1, source_target_pairs={{0,16},{16,0},{1,17},{17,1},{2,18},{18,2},{3,19},{19,3},{4,20},{20... | collective-permute-start | bytes 3538952 | tf_op jit(solution)/shard_map/ppermute | solution.py:47
  34.3 53.0 %copy-start.1 = (bf16[768,768]{1,0:T(8,128)(2,1)}, bf16[768,768]{1,0:T(8,128)(2,1)S(1)}, u32[]{:S(2)}) copy-start(bf16[768,768]{1,0:T(8,128)(2,1)S(1)} %pad_maximum_fusion.refs_4_) | copy-start | bytes 3538948
  34.4 31.6 %collective-permute-start.5 = (bf16[768,768]{1,0:T(8,128)(2,1)S(1)}, bf16[768,768]{1,0:T(8,128)(2,1)}, u32[]{:S(2)}, u32[]{:S(2)}) collective-permute-start(bf16[768,768]{1,0:T(8,128)(2,1)S(1)} %pad_maximum_fusion.refs_4_), channel_id=1, source_target_pairs={{0,1},{1,2},{2,3},{3,0},{8,11},{9,8},{10,9},{11,10},{4,5},{5,6},{6... | collective-permute-start | bytes 3538952 | tf_op jit(solution)/shard_map/ppermute | solution.py:212
  43.1 20.9 %collective-permute-start = (bf16[128,3072]{1,0:T(8,128)(2,1)}, bf16[128,3072]{1,0:T(8,128)(2,1)}, u32[]{:S(2)}, u32[]{:S(2)}) collective-permute-start(bf16[128,3072]{1,0:T(8,128)(2,1)} %bitcast_dynamic-update-slice_fusion.4.refs_0_), channel_id=1, source_target_pairs={{0,32},{32,64},{64,96},{96,0},{1,33},{33,65},{65,97},{97,1},{2,34}... | collective-permute-start | bytes 2359304 | tf_op jit(solution)/shard_map/ppermute | solution.py:47
  43.8 3.0 %collective-permute-start.16 = (bf16[2,128,768]{2,1,0:T(8,128)(2,1)}, bf16[2,128,768]{2,1,0:T(8,128)(2,1)}, u32[]{:S(2)}, u32[]{:S(2)}) collective-permute-start(bf16[2,128,768]{2,1,0:T(8,128)(2,1)} %collective-permute-done.12.refs_11_.refs_19_), channel_id=1, source_target_pairs={{0,8},{8,0},{1,9},{9,1},{2,10},{10,2},{3,11},{11,3},{4,12},{12,4},... | collective-permute-start | bytes 1179656 | tf_op jit(solution)/shard_map/ppermute | solution.py:47
  44.9 21.1 %collective-permute-start.1 = (bf16[128,3072]{1,0:T(8,128)(2,1)}, bf16[128,3072]{1,0:T(8,128)(2,1)}, u32[]{:S(2)}, u32[]{:S(2)}) collective-permute-start(bf16[128,3072]{1,0:T(8,128)(2,1)} %bitcast_dynamic-update-slice_fusion.4.refs_0_), channel_id=1, source_target_pairs={{0,96},{32,0},{64,32},{96,64},{1,97},{33,1},{65,33},{97,65},{2,98}... | collective-permute-start | bytes 2359304 | tf_op jit(solution)/shard_map/ppermute | solution.py:47
  46.8 39.6 %collective-permute-start.15 = (bf16[2,384,768]{2,1,0:T(8,128)(2,1)S(1)}, bf16[2,384,768]{2,1,0:T(8,128)(2,1)S(1)}, u32[]{:S(2)}, u32[]{:S(2)}) collective-permute-start(bf16[2,384,768]{2,1,0:T(8,128)(2,1)S(1)} %constant_dynamic-update-slice_fusion.refs_10_.refs_18_), channel_id=1, source_target_pairs={{0,8},{8,0},{1,9},{9,1},{2,10},{10,2},{3,11},{11,3},{4,12},{12,4},... | collective-permute-start | bytes 3538952 | tf_op jit(solution)/shard_map/ppermute | solution.py:47
  64.0 15.3 %collective-permute-start.6 = (bf16[384,768]{1,0:T(8,128)(2,1)S(1)}, bf16[384,768]{1,0:T(8,128)(2,1)S(1)}, u32[]{:S(2)}, u32[]{:S(2)}) collective-permute-start(bf16[384,768]{1,0:T(8,128)(2,1)S(1)} %constant_dynamic-slice_fusion), channel_id=1, source_target_pairs={{0,2},{1,3},{2,0},{3,1},{4,6},{5,7},{6,4},{7,5},{8,10},{9,11},{10,... | collective-permute-start | bytes 1769480 | tf_op jit(solution)/shard_map/ppermute | solution.py:47
  64.0 23.3 %copy-start.3 = (bf16[2,384,768]{2,1,0:T(8,128)(2,1)}, bf16[2,384,768]{2,1,0:T(8,128)(2,1)S(1)}, u32[]{:S(2)}) copy-start(bf16[2,384,768]{2,1,0:T(8,128)(2,1)S(1)} %collective-permute-done.13.refs_12_.refs_20_) | copy-start | bytes 3538948
  64.0 22.5 %collective-permute-start.17 = (bf16[2,384,768]{2,1,0:T(8,128)(2,1)S(1)}, bf16[2,384,768]{2,1,0:T(8,128)(2,1)S(1)}, u32[]{:S(2)}, u32[]{:S(2)}) collective-permute-start(bf16[2,384,768]{2,1,0:T(8,128)(2,1)S(1)} %collective-permute-done.13.refs_12_.refs_20_), channel_id=1, source_target_pairs={{0,8},{8,0},{1,9},{9,1},{2,10},{10,2},{3,11},{11,3},{4,12},{12,4},... | collective-permute-start | bytes 3538952 | tf_op jit(solution)/shard_map/ppermute | solution.py:47
  65.9 21.4 %collective-permute-start.7 = (bf16[768,768]{1,0:T(8,128)(2,1)}, bf16[768,768]{1,0:T(8,128)(2,1)S(1)}, u32[]{:S(2)}, u32[]{:S(2)}) collective-permute-start(bf16[768,768]{1,0:T(8,128)(2,1)} %collective-permute-done.5.refs_5_), channel_id=1, source_target_pairs={{0,8},{8,0},{1,9},{9,1},{2,10},{10,2},{3,11},{11,3},{4,12},{12,4},... | collective-permute-start | bytes 3538952 | tf_op jit(solution)/shard_map/ppermute | solution.py:47
  66.0 20.4 %collective-permute-start.2 = (bf16[128,3072]{1,0:T(8,128)(2,1)}, bf16[128,3072]{1,0:T(8,128)(2,1)S(1)}, u32[]{:S(2)}, u32[]{:S(2)}) collective-permute-start(bf16[128,3072]{1,0:T(8,128)(2,1)} %bitcast_dynamic-update-slice_fusion.4.refs_0_), channel_id=1, source_target_pairs={{0,64},{32,96},{64,0},{96,32},{1,65},{33,97},{65,1},{97,33},{2,66}... | collective-permute-start | bytes 2359304 | tf_op jit(solution)/shard_map/ppermute | solution.py:47
  79.3 7.1 %collective-permute-start.8 = (bf16[384,768]{1,0:T(8,128)(2,1)S(1)}, bf16[384,768]{1,0:T(8,128)(2,1)S(1)}, u32[]{:S(2)}, u32[]{:S(2)}) collective-permute-start(bf16[384,768]{1,0:T(8,128)(2,1)S(1)} %collective-permute-done.6.refs_6_), channel_id=1, source_target_pairs={{0,8},{8,0},{1,9},{9,1},{2,10},{10,2},{3,11},{11,3},{4,12},{12,4},... | collective-permute-start | bytes 1769480 | tf_op jit(solution)/shard_map/ppermute | solution.py:47
  121.7 5.5 %collective-permute-start.18 = (bf16[128,768]{1,0:T(8,128)(2,1)}, bf16[128,768]{1,0:T(8,128)(2,1)S(1)}, u32[]{:S(2)}, u32[]{:S(2)}) collective-permute-start(bf16[128,768]{1,0:T(8,128)(2,1)} %get-tuple-element.10), channel_id=1, source_target_pairs={{0,96},{32,0},{64,32},{96,64},{1,97},{33,1},{65,33},{97,65},{2,98}... | collective-permute-start | bytes 589832 | tf_op jit(solution)/shard_map/ppermute | solution.py:47
  122.9 5.9 %collective-permute-start.19 = (bf16[128,768]{1,0:T(8,128)(2,1)}, bf16[128,768]{1,0:T(8,128)(2,1)S(1)}, u32[]{:S(2)}, u32[]{:S(2)}) collective-permute-start(bf16[128,768]{1,0:T(8,128)(2,1)} %get-tuple-element.11), channel_id=1, source_target_pairs={{0,32},{32,64},{64,96},{96,0},{1,33},{33,65},{65,97},{97,1},{2,34}... | collective-permute-start | bytes 589832 | tf_op jit(solution)/shard_map/ppermute | solution.py:47
  123.2 10.3 %collective-permute-start.20 = (bf16[128,768]{1,0:T(8,128)(2,1)}, bf16[128,768]{1,0:T(8,128)(2,1)S(1)}, u32[]{:S(2)}, u32[]{:S(2)}) collective-permute-start(bf16[128,768]{1,0:T(8,128)(2,1)} %get-tuple-element.12), channel_id=1, source_target_pairs={{0,64},{32,96},{64,0},{96,32},{1,65},{33,97},{65,1},{97,33},{2,66}... | collective-permute-start | bytes 589832 | tf_op jit(solution)/shard_map/ppermute | solution.py:47
  (13 other events, 43.6 us)

commit v2 on v0

v2 whole, which is shorter than its diff:
```python
import math

import jax
import jax.numpy as jnp
from jax import lax
from jax.experimental import pallas as pl
from jax.experimental.pallas import tpu as pltpu
from jax.sharding import Mesh
from jax.sharding import PartitionSpec as P

HDIM = 64
BLOCK = 128
NORM_FLOOR = 0.25
EXP2_SCALE = HDIM**-0.5 * math.log2(math.e)
ROW_BLOCK = 384
KEY_CHUNK = 256
GROUPS = ((0, 1, 2), (3, 4, 5), (6, 7, 8), (9, 10, 11))
LANES = 128
COLUMN_BLOCK = 256
SEQ = ("z", "yh", "co")
FSDP = ("yl", "x")
Z, X = 4, 4


def dequantize(weight_codes, block_scales):
    row_count, column_count = weight_codes.shape
    blocked = weight_codes.astype(jnp.float32).reshape(
        row_count // BLOCK, BLOCK, column_count // BLOCK, BLOCK
    )
    return (
        (blocked * block_scales[:, None, :, None])
        .reshape(row_count, column_count)
        .astype(jnp.bfloat16)
    )


def shift(value, axis, by, size):
    return lax.ppermute(value, axis, [(i, (i + by) % size) for i in range(size)])


def prepare(position, keys, values, gain, steps):
    count, features = keys.shape
    share = features // Z

    def body(position_ref, key_ref, value_ref, gain_ref, *out_refs):
        for by, out_ref in zip(steps, out_refs):
            at = pl.ds(pl.multiple_of(((position_ref[0] + by) % Z) * share, LANES), share)
            turned = key_ref[:, at].astype(jnp.float32).T.reshape(share // HDIM, HDIM, count)
            centred = turned - jnp.mean(turned, axis=1, keepdims=True)
            spread = jnp.mean(centred * centred, axis=1, keepdims=True)
            normed = (centred * lax.rsqrt(spread + NORM_FLOOR)).reshape(share, count)
            out_ref[0] = (normed.T * gain_ref[:, at]).astype(jnp.bfloat16)
            out_ref[1] = value_ref[:, at]

    whole = pl.BlockSpec(memory_space=pltpu.VMEM)
    return pl.pallas_call(
        body,
        in_specs=[pl.BlockSpec(memory_space=pltpu.SMEM), whole, whole, whole],
        out_specs=[whole for _ in steps],
        out_shape=[pltpu.VMEM((2, count, share), jnp.bfloat16) for _ in steps],
    )(position, keys, values, gain.reshape(1, features))


def assemble(position, pieces, steps):
    count, share = pieces[0].shape

    def body(position_ref, *refs):
        out_ref = refs[-1]
        for by, ref in zip(steps, refs[:-1]):
            at = pl.ds(pl.multiple_of(((position_ref[0] + by) % Z) * share, LANES), share)
            out_ref[0, :, at] = ref[...]

    whole = pl.BlockSpec(memory_space=pltpu.VMEM)
    return pl.pallas_call(
        body,
        in_specs=[pl.BlockSpec(memory_space=pltpu.SMEM)] + [whole for _ in pieces],
        out_specs=whole,
        out_shape=jax.ShapeDtypeStruct((1, count, share * Z), jnp.bfloat16),
    )(position, *[in_vmem(p) for p in pieces])


def project_and_attend(order, tokens, weights, pairs, gain):
    token_counts = [t.shape[0] for t in tokens]
    key_counts = [p.shape[1] for p in pairs]
    total, keys = sum(token_counts), sum(key_counts)
    features, columns = tokens[0].shape[1], weights[0].shape[1]
    heads, block_heads = columns // HDIM, COLUMN_BLOCK // HDIM
    nt, nw, nk = len(tokens), len(weights), len(pairs)

    def body(order_ref, *refs):
        token_refs, refs = refs[:nt], refs[nt:]
        weight_refs, refs = refs[:nw], refs[nw:]
        pair_refs, refs = refs[:nk], refs[nk:]
        gain_ref, refs = refs[0], refs[1:]
        out_refs, refs = refs[:nt], refs[nt:]
        sorted_ref, query_ref, value_t, score_a, score_b, top_a, top_b, out_t = refs
        for j in range(features // ROW_BLOCK):
            src = pl.ds(pl.multiple_of(order_ref[j] * ROW_BLOCK, LANES), ROW_BLOCK)
            at = 0
            for t, ref in enumerate(token_refs):
                sorted_ref[at : at + token_counts[t], j * ROW_BLOCK : (j + 1) * ROW_BLOCK] = ref[:, src]
                at += token_counts[t]

        def project(i, carry):
            cols = pl.ds(pl.multiple_of(i * COLUMN_BLOCK, COLUMN_BLOCK), COLUMN_BLOCK)
            queries = jnp.dot(
                sorted_ref[...],
                jnp.concatenate([w[:, cols] for w in weight_refs], axis=0),
                preferred_element_type=jnp.float32,
            )
            turned = queries.T.reshape(block_heads, HDIM, total)
            centred = turned - jnp.mean(turned, axis=1, keepdims=True)
            spread = jnp.mean(centred * centred, axis=1, keepdims=True)
            gains = gain_ref[cols, :].reshape(block_heads, HDIM, 1)
            normed = (centred * lax.rsqrt(spread + NORM_FLOOR) * gains).astype(jnp.bfloat16)
            scaled = normed.astype(jnp.float32) * EXP2_SCALE
            high = scaled.astype(jnp.bfloat16)
            low = (scaled - high.astype(jnp.float32)).astype(jnp.bfloat16)
            nothing = jnp.zeros((HDIM, total), jnp.bfloat16)
            for h in range(block_heads):
                at = i * block_heads + h
                for part, value in enumerate((high[h], low[h])):
                    up, down = (value, nothing) if h % 2 == 0 else (nothing, value)
                    query_ref[at, part * LANES : part * LANES + HDIM] = up
                    query_ref[at, part * LANES + HDIM : (part + 1) * LANES] = down
            at = 0
            for ref in pair_refs:
                n = ref.shape[1]
                value_t[cols, at : at + n] = ref[1, :, cols].T
                at += n
            return carry

        lax.fori_loop(0, columns // COLUMN_BLOCK, project, 0)

        def scores(h, score_ref, top_ref):
            lanes = pl.ds(pl.multiple_of((h // 2) * LANES, LANES), LANES)
            at, top = 0, None
            for group in GROUPS:
                key = jnp.concatenate([pair_refs[g][0, :, lanes] for g in group], axis=0)
                n = key.shape[0]
                score = jnp.dot(
                    jnp.concatenate([key, key], axis=1),
                    query_ref[h],
                    preferred_element_type=jnp.float32,
                )
                score_ref[at : at + n] = score
                best = jnp.max(score.reshape(n // 8, 8, total), axis=0)
                top = best if top is None else jnp.maximum(top, best)
                at += n
            top_ref[...] = top

        def finish(h, score_ref, top_ref):
            rows = pl.ds(pl.multiple_of(h * HDIM, HDIM), HDIM)
            top = jnp.max(top_ref[...], axis=0, keepdims=True)
            sums, blend = None, None
            for at in range(0, keys, KEY_CHUNK):
                prob = jnp.exp2(score_ref[at : at + KEY_CHUNK] - top)
                part = jnp.sum(prob.reshape(KEY_CHUNK // 8, 8, total), axis=0)
                sums = part if sums is None else sums + part
                more = jnp.dot(
                    value_t[rows, at : at + KEY_CHUNK],
                    prob.astype(jnp.bfloat16),
                    preferred_element_type=jnp.float32,
                )
                blend = more if blend is None else blend + more
            out_t[rows] = blend / jnp.sum(sums, axis=0, keepdims=True)

        scores(0, score_a, top_a)

        def pair(p, carry):
            @pl.when(p >= 0)
            def _():
                finish(2 * p, score_a, top_a)
                scores(2 * p + 1, score_b, top_b)

            @pl.when(p < heads)
            def _():
                finish(2 * p + 1, score_b, top_b)
                scores(jnp.minimum(2 * p + 2, heads - 1), score_a, top_a)

            return carry

        lax.fori_loop(0, heads // 2, pair, 0)
        at = 0
        for t, ref in enumerate(out_refs):
            ref[...] = out_t[:, at : at + token_counts[t]].T.astype(jnp.bfloat16)
            at += token_counts[t]

    inside = pl.BlockSpec(memory_space=pltpu.VMEM)
    operands = [in_vmem(v) for v in (*tokens, *weights, *pairs, gain)]
    return pl.pallas_call(
        body,
        in_specs=[pl.BlockSpec(memory_space=pltpu.SMEM)] + [inside] * len(operands),
        out_specs=[inside] * nt,
        scratch_shapes=[
            pltpu.VMEM((total, features), jnp.bfloat16),
            pltpu.VMEM((heads, 2 * LANES, total), jnp.bfloat16),
            pltpu.VMEM((columns, keys), jnp.bfloat16),
            pltpu.VMEM((keys, total), jnp.float32),
            pltpu.VMEM((keys, total), jnp.float32),
            pltpu.VMEM((8, total), jnp.float32),
            pltpu.VMEM((8, total), jnp.float32),
            pltpu.VMEM((columns, total), jnp.float32),
        ],
        out_shape=[pltpu.VMEM((t, columns), jnp.bfloat16) for t in token_counts],
        compiler_params=pltpu.CompilerParams(vmem_limit_bytes=24 << 20),
    )(order, *operands)


def in_vmem(value):
    return pltpu.with_memory_space_constraint(value, pltpu.VMEM)


def layer(patches, weight_codes, block_scales, key_proj, value_proj, query_gain, key_gain):
    _, features = patches.shape[1:]
    rows = weight_codes.shape[0]
    share = features // Z
    z, co, yl, x = (lax.axis_index(a) for a in ("z", "co", "yl", "x"))
    position = z.astype(jnp.int32).reshape(1)
    steps = (0, 1, 3, 2)

    own = dequantize(
        lax.dynamic_slice(weight_codes, (0, z * share), (rows, share)),
        lax.dynamic_slice(
            block_scales, (0, z * (share // BLOCK)), (rows // BLOCK, share // BLOCK)
        ),
    )
    y_moves = []
    for y in range(4):
        for core, by in ((0, 1), (1, 3)):
            to = (y + by) % 4
            y_moves.append((((y // 2) * 2 + core) * 2 + y % 2, ((to // 2) * 2 + core) * 2 + to % 2))
    x_moves = [
        (core * X + i, core * X + (i + by) % X) for core, by in ((0, 1), (1, 3)) for i in range(X)
    ]
    other = lax.ppermute(own, ("yh", "co", "yl"), y_moves)
    near_own = lax.ppermute(own, ("co", "x"), x_moves)
    near_other = lax.ppermute(other, ("co", "x"), x_moves)
    mine_far = shift(jnp.where(co == 0, own, other), "x", 2, X)
    weights = [
        own,
        other,
        near_own,
        near_other,
        mine_far,
        shift(near_own, "co", 1, 2),
        shift(near_other, "co", 1, 2),
        shift(mine_far, "co", 1, 2),
    ]

    near, first, third, second = prepare(position, key_proj[0], value_proj[0], key_gain, steps)
    sent = [shift(piece, "z", by, Z) for by, piece in ((1, first), (3, third), (2, second))]
    near_y = shift(near, "yh", 1, 2)
    middle = jnp.concatenate(sent[:2], axis=1)
    middle_y = shift(middle, "yh", 1, 2)
    far = sent[2]
    far_y = shift(far, "yh", 1, 2)
    pieces = {
        "near": near,
        "middle": middle,
        "far": far,
        "neary": near_y,
        "middley": middle_y,
        "fary": far_y,
    }
    pairs = list(pieces.values())
    pairs += [shift(piece, "co", 1, 2) for piece in pieces.values()]

    back = jnp.where(co == 0, 3, 1)
    order = jnp.stack(
        [
            a * X + b % X
            for a, b in (
                (yl, x),
                (1 - yl, x),
                (yl, x + back),
                (1 - yl, x + back),
                ((yl + co) % 2, x + 2),
                (yl, x + 4 - back),
                (1 - yl, x + 4 - back),
                ((yl + 1 - co) % 2, x + 2),
            )
        ]
    ).astype(jnp.int32)
    arrived = {by: shift(patches[0], "z", by, Z) for by in (1, 3, 2)}
    gain = lax.dynamic_slice(query_gain, (z * share,), (share,)).reshape(share, 1)
    done = {}
    done[1], done[3] = project_and_attend(order, [arrived[1], arrived[3]], weights, pairs, gain)
    done[2], done[0] = project_and_attend(order, [arrived[2], patches[0]], weights, pairs, gain)
    pieces = [shift(done[by], "z", Z - by, Z) if by else done[by] for by in steps]
    return assemble(position, pieces, steps)


def solution(mesh):
    split = Mesh(mesh.devices.reshape(Z, 2, 2, 2, X), ("z", "yh", "co", "yl", "x"))
    placed = (
        P(FSDP, SEQ, None),
        P(FSDP, None),
        P(FSDP, None),
        P(FSDP, SEQ, None),
        P(FSDP, SEQ, None),
        P(),
        P(),
    )
    return jax.shard_map(
        layer, mesh=split, in_specs=placed, out_specs=P(FSDP, SEQ, None), check_vma=False
    )
```

time: 282 us -> 118 us (0.42)
  waiting for transfers between devices: 152 us -> 27.6 us
  blocking collectives: 39.5 us -> 0 us
  Pallas kernels: 0 us -> 30.9 us
  matrix products: 28 us -> 0 us
  starting transfers between devices: 18 us -> 39.2 us
  other arithmetic: 16.6 us -> 1.64 us
  between operations: 13.6 us -> 0.18 us
  local copies, waits for them, and re-layouts: 13.6 us -> 17.3 us
    reduce_scatter x1 -> x0, waiting for transfers between devices: 119 us -> none  [per_device(): lax.psum_scatter(jnp.dot(group_rows, local_weight, preferred_element_type...]
    all_to_all x3 -> x0, blocking collectives: 39.5 us -> none  [the longest x2 21.8 us: exchange_in_order(): whole = lax.all_to_all(whole, axes[k], k, k, tiled=True)]
    ppermute x0 -> x25, starting transfers between devices: none -> 39.2 us  [the longest x22 31.6 us: shift(): lax.ppermute(value, axis, [(i, (i + by) % size) for i in range(size)])]
    all_to_all x3 -> x0, waiting for transfers between devices: 32.8 us -> none  [the longest x1 12.8 us: per_device(): lax.all_to_all(query_view, SEQ, split_axis=2, concat_axis=1, tiled=True)]
    pallas_call x0 -> x4, Pallas kernels: none -> 30.9 us  [the longest x2 27.5 us: project_and_attend(): pl.pallas_call(body, in_specs=[pl.BlockSpec(memory_space=pltpu.SMEM)] + [...]
    dot_general x9 -> x0, matrix products: 28 us -> none  [the longest x4 13.2 us: attend_block(): jnp.einsum('iths,ishd->ithd', probability.astype(jnp.bfloat16), value_vie...]
    ppermute x0 -> x25, waiting for transfers between devices: none -> 27.6 us  [the longest x22 23.4 us: shift(): lax.ppermute(value, axis, [(i, (i + by) % size) for i in range(size)])]
    all_to_all x3 -> x0, starting transfers between devices: 18 us -> none  [the longest x1 9.47 us: per_device(): lax.all_to_all(key_norm, SEQ, split_axis=2, concat_axis=1, tiled=True)]
  transfers between devices with their start and end apart: 4 -> 25, of which waited for: 4 -> 9; matrix products, arithmetic and copies ran while one was open for 3% -> 3% of each run, Pallas kernels for 0% -> 24%
where the time goes in v2:
time: 118 us; the launch traced here: 117 us
  starting transfers between devices  39.2 us (33%)
  Pallas kernels  30.9 us (26%)
  waiting for transfers between devices  27.6 us (23%)
  local copies, waits for them, and re-layouts  17.3 us (15%)
  other arithmetic  1.64 us (1%)
    ppermute x22, starting transfers between devices, shift(): lax.ppermute(value, axis, [(i, (i + by) % size) for i in range(size)])  31.6 us
    pallas_call x2, Pallas kernels, project_and_attend(): pl.pallas_call(body, in_specs=[pl.BlockSpec(memory_space=pltpu.SMEM)] + [...  27.5 us
    ppermute x22, waiting for transfers between devices, shift(): lax.ppermute(value, axis, [(i, (i + by) % size) for i in range(size)])  23.4 us
    unnamed x47, local copies, waits for them, and re-layouts  15 us
    ppermute x1, waiting for transfers between devices, layer(): near_other = lax.ppermute(other, ('co', 'x'), x_moves)  4.19 us
    ppermute x1, starting transfers between devices, layer(): other = lax.ppermute(own, ('yh', 'co', 'yl'), y_moves)  2.8 us
    ppermute x1, starting transfers between devices, layer(): near_own = lax.ppermute(own, ('co', 'x'), x_moves)  2.48 us
    pallas_call x1, Pallas kernels, prepare(): pl.pallas_call(body, in_specs=[pl.BlockSpec(memory_space=pltpu.SMEM), who...  2.45 us
  transfers between devices with their start and end apart: 25, of which 9 were waited for; matrix products, arithmetic and copies ran while one was open for 3% of the time, Pallas kernels for 24%

profile of v2, /device:TPU:1, one launch (start us, length us, event | category | flops | bytes accessed | tf_op | source)
XLA Modules:
  0.0 116.8 jit_solution(16501167745888196918)
XLA Ops:
  0.0 2.5 %shard_map.73 = (bf16[2,128,768]{2,1,0:T(8,128)(2,1)S(1)}, bf16[2,128,768]{2,1,0:T(8,128)(2,1)S(1)}, bf16[2,128,768]{2,1,0:T(8,128)(2,1)S(1)}, bf16[2,128,768]{2,1,0:T(8,128)(2,1)S(1)}) custom-call(s32[1]{0:T(128)} %bitcast.position_ref, bf16[128,3072]{1,0:T(8,128)(2,1)} %bitcast.20, bf16[128,3072]{1,0:T(8,128)(2,1)} %bitcast.21, f32[1,3072]{1,0:T(1,128)} %bitcast.22), custom_call_target="tpu_custom_call" | custom-call | tf_op jit(solution)/shard_map/pallas_call | solution.py:56
  2.5 2.5 %collective-permute-start.8 = (bf16[2,128,768]{2,1,0:T(8,128)(2,1)S(1)}, bf16[2,128,768]{2,1,0:T(8,128)(2,1)S(1)}, u32[]{:S(2)}, u32[]{:S(2)}) collective-permute-start(bf16[2,128,768]{2,1,0:T(8,128)(2,1)S(1)} %get-tuple-element.14), channel_id=1, source_target_pairs={{0,32},{32,64},{64,96},{96,0},{1,33},{33,65},{65,97},{97,1},{2,34}... | collective-permute-start | bytes 1179656 | tf_op jit(solution)/shard_map/ppermute | solution.py:38
  5.0 2.2 %collective-permute-start.9 = (bf16[2,128,768]{2,1,0:T(8,128)(2,1)S(1)}, bf16[2,128,768]{2,1,0:T(8,128)(2,1)}, u32[]{:S(2)}, u32[]{:S(2)}) collective-permute-start(bf16[2,128,768]{2,1,0:T(8,128)(2,1)S(1)} %get-tuple-element.15), channel_id=1, source_target_pairs={{0,96},{32,0},{64,32},{96,64},{1,97},{33,1},{65,33},{97,65},{2,98}... | collective-permute-start | bytes 1179656 | tf_op jit(solution)/shard_map/ppermute | solution.py:38
  7.4 1.6 %fusion.refs_2_ = bf16[384,768]{1,0:T(8,128)(2,1)S(1)} fusion(f32[48,8,6,128]{3,2,1,0:T(8,128)S(1)} %bitcast.19, s32[384,3072]{1,0:T(8,128)} %param.8, s32[]{:T(128)S(6)} %select_n.61), kind=kLoop, calls=%fused_computation.1 | loop fusion | flops 884736 | bytes 2949124 | tf_op jit(solution)/shard_map/convert_element_type | solution.py:33
  9.0 2.8 %collective-permute-start.1 = (bf16[384,768]{1,0:T(8,128)(2,1)S(1)}, bf16[384,768]{1,0:T(8,128)(2,1)S(1)}, u32[]{:S(2)}, u32[]{:S(2)}) collective-permute-start(bf16[384,768]{1,0:T(8,128)(2,1)S(1)} %fusion.refs_2_), channel_id=1, source_target_pairs={{0,4},{8,28},{4,16},{12,8},{16,20},{24,12},{20,0},{28,24},{1,5},{9... | collective-permute-start | bytes 1769480 | tf_op jit(solution)/shard_map/ppermute | solution.py:236
  13.4 2.5 %collective-permute-done.8 = bf16[2,128,768]{2,1,0:T(8,128)(2,1)S(1)} collective-permute-done((bf16[2,128,768]{2,1,0:T(8,128)(2,1)S(1)}, bf16[2,128,768]{2,1,0:T(8,128)(2,1)S(1)}, u32[]{:S(2)}, u32[]{:S(2)}) %collective-permute-start.8) | collective-permute-done | bytes 393248 | tf_op jit(solution)/shard_map/ppermute | solution.py:38
  17.2 2.5 %collective-permute-start.2 = (bf16[384,768]{1,0:T(8,128)(2,1)S(1)}, bf16[384,768]{1,0:T(8,128)(2,1)}, u32[]{:S(2)}, u32[]{:S(2)}) collective-permute-start(bf16[384,768]{1,0:T(8,128)(2,1)S(1)} %fusion.refs_2_), channel_id=1, source_target_pairs={{0,1},{1,2},{2,3},{3,0},{8,11},{9,8},{10,9},{11,10},{4,5},{5,6},{6... | collective-permute-start | bytes 1769480 | tf_op jit(solution)/shard_map/ppermute | solution.py:237
  19.7 5.6 %collective-permute-done.10.refs_12_ = bf16[2,128,768]{2,1,0:T(8,128)(2,1)S(1)} collective-permute-done((bf16[2,128,768]{2,1,0:T(8,128)(2,1)S(1)}, bf16[2,128,768]{2,1,0:T(8,128)(2,1)S(1)}, u32[]{:S(2)}, u32[]{:S(2)}) %collective-permute-start.10) | collective-permute-done | bytes 393248 | tf_op jit(solution)/shard_map/ppermute | solution.py:38
  25.3 2.9 %collective-permute-start.13 = (bf16[2,128,768]{2,1,0:T(8,128)(2,1)S(1)}, bf16[2,128,768]{2,1,0:T(8,128)(2,1)}, u32[]{:S(2)}, u32[]{:S(2)}) collective-permute-start(bf16[2,128,768]{2,1,0:T(8,128)(2,1)S(1)} %collective-permute-done.10.refs_12_), channel_id=1, source_target_pairs={{0,16},{16,0},{1,17},{17,1},{2,18},{18,2},{3,19},{19,3},{4,20},{20... | collective-permute-start | bytes 1179656 | tf_op jit(solution)/shard_map/ppermute | solution.py:38
  28.2 1.6 %collective-permute-start.20 = (bf16[128,3072]{1,0:T(8,128)(2,1)}, bf16[128,3072]{1,0:T(8,128)(2,1)}, u32[]{:S(2)}, u32[]{:S(2)}) collective-permute-start(bf16[128,3072]{1,0:T(8,128)(2,1)} %bitcast.9.refs_1_), channel_id=1, source_target_pairs={{0,32},{32,64},{64,96},{96,0},{1,33},{33,65},{65,97},{97,1},{2,34}... | collective-permute-start | bytes 2359304 | tf_op jit(solution)/shard_map/ppermute | solution.py:38
  31.6 4.2 %collective-permute-start.17 = (bf16[2,128,768]{2,1,0:T(8,128)(2,1)}, bf16[2,128,768]{2,1,0:T(8,128)(2,1)S(1)}, u32[]{:S(2)}, u32[]{:S(2)}) collective-permute-start(bf16[2,128,768]{2,1,0:T(8,128)(2,1)} %collective-permute-done.11.refs_13_), channel_id=1, source_target_pairs={{0,8},{8,0},{1,9},{9,1},{2,10},{10,2},{3,11},{11,3},{4,12},{12,4},... | collective-permute-start | bytes 1179656 | tf_op jit(solution)/shard_map/ppermute | solution.py:38
  37.9 1.5 %collective-permute-start.16 = (bf16[2,128,768]{2,1,0:T(8,128)(2,1)S(1)}, bf16[2,128,768]{2,1,0:T(8,128)(2,1)S(1)}, u32[]{:S(2)}, u32[]{:S(2)}) collective-permute-start(bf16[2,128,768]{2,1,0:T(8,128)(2,1)S(1)} %collective-permute-done.10.refs_12_), channel_id=1, source_target_pairs={{0,8},{8,0},{1,9},{9,1},{2,10},{10,2},{3,11},{11,3},{4,12},{12,4},... | collective-permute-start | bytes 1179656 | tf_op jit(solution)/shard_map/ppermute | solution.py:38
  40.2 2.7 %collective-permute-start.4 = (bf16[384,768]{1,0:T(8,128)(2,1)S(1)}, bf16[384,768]{1,0:T(8,128)(2,1)}, u32[]{:S(2)}, u32[]{:S(2)}) collective-permute-start(bf16[384,768]{1,0:T(8,128)(2,1)S(1)} %broadcast_select_fusion), channel_id=1, source_target_pairs={{0,2},{1,3},{2,0},{3,1},{4,6},{5,7},{6,4},{7,5},{8,10},{9,11},{10,... | collective-permute-start | bytes 1769480 | tf_op jit(solution)/shard_map/ppermute | solution.py:38
  44.0 1.3 %collective-permute-done.20.refs_0_ = bf16[128,3072]{1,0:T(8,128)(2,1)} collective-permute-done((bf16[128,3072]{1,0:T(8,128)(2,1)}, bf16[128,3072]{1,0:T(8,128)(2,1)}, u32[]{:S(2)}, u32[]{:S(2)}) %collective-permute-start.20) | collective-permute-done | bytes 786464 | tf_op jit(solution)/shard_map/ppermute | solution.py:38
  45.3 2.3 %collective-permute-start.3 = (bf16[384,768]{1,0:T(8,128)(2,1)S(1)}, bf16[384,768]{1,0:T(8,128)(2,1)}, u32[]{:S(2)}, u32[]{:S(2)}) collective-permute-start(bf16[384,768]{1,0:T(8,128)(2,1)S(1)} %collective-permute-done.1.refs_3_), channel_id=1, source_target_pairs={{0,1},{1,2},{2,3},{3,0},{8,11},{9,8},{10,9},{11,10},{4,5},{5,6},{6... | collective-permute-start | bytes 1769480 | tf_op jit(solution)/shard_map/ppermute | solution.py:238
  47.6 1.8 %collective-permute-done.21.refs_1_ = bf16[128,3072]{1,0:T(8,128)(2,1)} collective-permute-done((bf16[128,3072]{1,0:T(8,128)(2,1)}, bf16[128,3072]{1,0:T(8,128)(2,1)}, u32[]{:S(2)}, u32[]{:S(2)}) %collective-permute-start.21) | collective-permute-done | bytes 786464 | tf_op jit(solution)/shard_map/ppermute | solution.py:38
  49.4 2.2 %collective-permute-start.5 = (bf16[384,768]{1,0:T(8,128)(2,1)}, bf16[384,768]{1,0:T(8,128)(2,1)S(1)}, u32[]{:S(2)}, u32[]{:S(2)}) collective-permute-start(bf16[384,768]{1,0:T(8,128)(2,1)} %collective-permute-done.2.refs_4_), channel_id=1, source_target_pairs={{0,8},{8,0},{1,9},{9,1},{2,10},{10,2},{3,11},{11,3},{4,12},{12,4},... | collective-permute-start | bytes 1769480 | tf_op jit(solution)/shard_map/ppermute | solution.py:38
  51.6 6.0 %collective-permute-done.12.refs_14_ = bf16[2,256,768]{2,1,0:T(8,128)(2,1)S(1)} collective-permute-done((bf16[2,256,768]{2,1,0:T(8,128)(2,1)S(1)}, bf16[2,256,768]{2,1,0:T(8,128)(2,1)S(1)}, u32[]{:S(2)}, u32[]{:S(2)}) %collective-permute-start.12) | collective-permute-done | bytes 786464 | tf_op jit(solution)/shard_map/ppermute | solution.py:38
  59.4 4.2 %collective-permute-done.3.refs_5_ = bf16[384,768]{1,0:T(8,128)(2,1)} collective-permute-done((bf16[384,768]{1,0:T(8,128)(2,1)S(1)}, bf16[384,768]{1,0:T(8,128)(2,1)}, u32[]{:S(2)}, u32[]{:S(2)}) %collective-permute-start.3) | collective-permute-done | bytes 589856 | tf_op jit(solution)/shard_map/ppermute | solution.py:238
  74.1 13.8 %shard_map.75 = (bf16[128,768]{1,0:T(8,128)(2,1)S(1)}, bf16[128,768]{1,0:T(8,128)(2,1)S(1)}) custom-call(s32[8]{0:T(128)S(1)} %stack.35.order_ref, bf16[128,3072]{1,0:T(8,128)(2,1)} %collective-permute-done.20.refs_0_, bf16[128,3072]{1,0:T(8,128)(2,1)} %collective-permute-done.21.refs_1_, bf16[384,768]{1,0:T(8,128)(2,1)S(1)} %fusion.refs_2_, ...), custom_call_target="tpu_custom_call" | custom-call | tf_op jit(solution)/shard_map/pallas_call | solution.py:191
  87.9 3.5 %collective-permute-start.22 = (bf16[128,768]{1,0:T(8,128)(2,1)S(1)}, bf16[128,768]{1,0:T(8,128)(2,1)S(1)}, u32[]{:S(2)}, u32[]{:S(2)}) collective-permute-start(bf16[128,768]{1,0:T(8,128)(2,1)S(1)} %get-tuple-element.18), channel_id=1, source_target_pairs={{0,96},{32,0},{64,32},{96,64},{1,97},{33,1},{65,33},{97,65},{2,98}... | collective-permute-start | bytes 589832 | tf_op jit(solution)/shard_map/ppermute | solution.py:38
  91.4 13.7 %shard_map.74 = (bf16[128,768]{1,0:T(8,128)(2,1)S(1)}, bf16[128,768]{1,0:T(8,128)(2,1)S(1)}) custom-call(s32[8]{0:T(128)S(1)} %stack.35.order_ref, bf16[128,3072]{1,0:T(8,128)(2,1)} %collective-permute-done.refs_0_, bf16[128,3072]{1,0:T(8,128)(2,1)} %bitcast.9.refs_1_, bf16[384,768]{1,0:T(8,128)(2,1)S(1)} %fusion.refs_2_, ...), custom_call_target="tpu_custom_call" | custom-call | tf_op jit(solution)/shard_map/pallas_call | solution.py:191
  105.8 1.4 %collective-permute-start.24 = (bf16[128,768]{1,0:T(8,128)(2,1)S(1)}, bf16[128,768]{1,0:T(8,128)(2,1)S(1)}, u32[]{:S(2)}, u32[]{:S(2)}) collective-permute-start(bf16[128,768]{1,0:T(8,128)(2,1)S(1)} %get-tuple-element.20), channel_id=1, source_target_pairs={{0,64},{32,96},{64,0},{96,32},{1,65},{33,97},{65,1},{97,33},{2,66}... | collective-permute-start | bytes 589832 | tf_op jit(solution)/shard_map/ppermute | solution.py:38
  108.6 4.5 %collective-permute-done.24.refs_3_ = bf16[128,768]{1,0:T(8,128)(2,1)S(1)} collective-permute-done((bf16[128,768]{1,0:T(8,128)(2,1)S(1)}, bf16[128,768]{1,0:T(8,128)(2,1)S(1)}, u32[]{:S(2)}, u32[]{:S(2)}) %collective-permute-start.24) | collective-permute-done | bytes 196640 | tf_op jit(solution)/shard_map/ppermute | solution.py:38
  (85 shorter events, 26.7 us)
Async XLA Ops:
  2.5 13.5 %collective-permute-start.8 = (bf16[2,128,768]{2,1,0:T(8,128)(2,1)S(1)}, bf16[2,128,768]{2,1,0:T(8,128)(2,1)S(1)}, u32[]{:S(2)}, u32[]{:S(2)}) collective-permute-start(bf16[2,128,768]{2,1,0:T(8,128)(2,1)S(1)} %get-tuple-element.14), channel_id=1, source_target_pairs={{0,32},{32,64},{64,96},{96,0},{1,33},{33,65},{65,97},{97,1},{2,34}... | collective-permute-start | bytes 1179656 | tf_op jit(solution)/shard_map/ppermute | solution.py:38
  5.0 12.2 %collective-permute-start.9 = (bf16[2,128,768]{2,1,0:T(8,128)(2,1)S(1)}, bf16[2,128,768]{2,1,0:T(8,128)(2,1)}, u32[]{:S(2)}, u32[]{:S(2)}) collective-permute-start(bf16[2,128,768]{2,1,0:T(8,128)(2,1)S(1)} %get-tuple-element.15), channel_id=1, source_target_pairs={{0,96},{32,0},{64,32},{96,64},{1,97},{33,1},{65,33},{97,65},{2,98}... | collective-permute-start | bytes 1179656 | tf_op jit(solution)/shard_map/ppermute | solution.py:38
  9.0 22.6 %collective-permute-start.1 = (bf16[384,768]{1,0:T(8,128)(2,1)S(1)}, bf16[384,768]{1,0:T(8,128)(2,1)S(1)}, u32[]{:S(2)}, u32[]{:S(2)}) collective-permute-start(bf16[384,768]{1,0:T(8,128)(2,1)S(1)} %fusion.refs_2_), channel_id=1, source_target_pairs={{0,4},{8,28},{4,16},{12,8},{16,20},{24,12},{20,0},{28,24},{1,5},{9... | collective-permute-start | bytes 1769480 | tf_op jit(solution)/shard_map/ppermute | solution.py:236
  11.8 13.4 %collective-permute-start.10 = (bf16[2,128,768]{2,1,0:T(8,128)(2,1)S(1)}, bf16[2,128,768]{2,1,0:T(8,128)(2,1)S(1)}, u32[]{:S(2)}, u32[]{:S(2)}) collective-permute-start(bf16[2,128,768]{2,1,0:T(8,128)(2,1)S(1)} %get-tuple-element.16), channel_id=1, source_target_pairs={{0,64},{32,96},{64,0},{96,32},{1,65},{33,97},{65,1},{97,33},{2,66}... | collective-permute-start | bytes 1179656 | tf_op jit(solution)/shard_map/ppermute | solution.py:38
  13.0 15.1 %collective-permute-start.11 = (bf16[2,128,768]{2,1,0:T(8,128)(2,1)S(1)}, bf16[2,128,768]{2,1,0:T(8,128)(2,1)}, u32[]{:S(2)}, u32[]{:S(2)}) collective-permute-start(bf16[2,128,768]{2,1,0:T(8,128)(2,1)S(1)} %get-tuple-element.13.refs_10_), channel_id=1, source_target_pairs={{0,16},{16,0},{1,17},{17,1},{2,18},{18,2},{3,19},{19,3},{4,20},{20... | collective-permute-start | bytes 1179656 | tf_op jit(solution)/shard_map/ppermute | solution.py:38
  15.9 13.9 %collective-permute-start.14 = (bf16[2,128,768]{2,1,0:T(8,128)(2,1)S(1)}, bf16[2,128,768]{2,1,0:T(8,128)(2,1)S(1)}, u32[]{:S(2)}, u32[]{:S(2)}) collective-permute-start(bf16[2,128,768]{2,1,0:T(8,128)(2,1)S(1)} %get-tuple-element.13.refs_10_), channel_id=1, source_target_pairs={{0,8},{8,0},{1,9},{9,1},{2,10},{10,2},{3,11},{11,3},{4,12},{12,4},... | collective-permute-start | bytes 1179656 | tf_op jit(solution)/shard_map/ppermute | solution.py:38
  17.2 19.8 %collective-permute-start.2 = (bf16[384,768]{1,0:T(8,128)(2,1)S(1)}, bf16[384,768]{1,0:T(8,128)(2,1)}, u32[]{:S(2)}, u32[]{:S(2)}) collective-permute-start(bf16[384,768]{1,0:T(8,128)(2,1)S(1)} %fusion.refs_2_), channel_id=1, source_target_pairs={{0,1},{1,2},{2,3},{3,0},{8,11},{9,8},{10,9},{11,10},{4,5},{5,6},{6... | collective-permute-start | bytes 1769480 | tf_op jit(solution)/shard_map/ppermute | solution.py:237
  25.3 12.6 %collective-permute-start.13 = (bf16[2,128,768]{2,1,0:T(8,128)(2,1)S(1)}, bf16[2,128,768]{2,1,0:T(8,128)(2,1)}, u32[]{:S(2)}, u32[]{:S(2)}) collective-permute-start(bf16[2,128,768]{2,1,0:T(8,128)(2,1)S(1)} %collective-permute-done.10.refs_12_), channel_id=1, source_target_pairs={{0,16},{16,0},{1,17},{17,1},{2,18},{18,2},{3,19},{19,3},{4,20},{20... | collective-permute-start | bytes 1179656 | tf_op jit(solution)/shard_map/ppermute | solution.py:38
  28.2 17.1 %collective-permute-start.20 = (bf16[128,3072]{1,0:T(8,128)(2,1)}, bf16[128,3072]{1,0:T(8,128)(2,1)}, u32[]{:S(2)}, u32[]{:S(2)}) collective-permute-start(bf16[128,3072]{1,0:T(8,128)(2,1)} %bitcast.9.refs_1_), channel_id=1, source_target_pairs={{0,32},{32,64},{64,96},{96,0},{1,33},{33,65},{65,97},{97,1},{2,34}... | collective-permute-start | bytes 2359304 | tf_op jit(solution)/shard_map/ppermute | solution.py:38
  30.6 18.8 %collective-permute-start.21 = (bf16[128,3072]{1,0:T(8,128)(2,1)}, bf16[128,3072]{1,0:T(8,128)(2,1)}, u32[]{:S(2)}, u32[]{:S(2)}) collective-permute-start(bf16[128,3072]{1,0:T(8,128)(2,1)} %bitcast.9.refs_1_), channel_id=1, source_target_pairs={{0,96},{32,0},{64,32},{96,64},{1,97},{33,1},{65,33},{97,65},{2,98}... | collective-permute-start | bytes 2359304 | tf_op jit(solution)/shard_map/ppermute | solution.py:38
  31.6 7.8 %collective-permute-start.17 = (bf16[2,128,768]{2,1,0:T(8,128)(2,1)}, bf16[2,128,768]{2,1,0:T(8,128)(2,1)S(1)}, u32[]{:S(2)}, u32[]{:S(2)}) collective-permute-start(bf16[2,128,768]{2,1,0:T(8,128)(2,1)} %collective-permute-done.11.refs_13_), channel_id=1, source_target_pairs={{0,8},{8,0},{1,9},{9,1},{2,10},{10,2},{3,11},{11,3},{4,12},{12,4},... | collective-permute-start | bytes 1179656 | tf_op jit(solution)/shard_map/ppermute | solution.py:38
  36.9 20.7 %collective-permute-start.12 = (bf16[2,256,768]{2,1,0:T(8,128)(2,1)S(1)}, bf16[2,256,768]{2,1,0:T(8,128)(2,1)S(1)}, u32[]{:S(2)}, u32[]{:S(2)}) collective-permute-start(bf16[2,256,768]{2,1,0:T(8,128)(2,1)S(1)} %constant_dynamic-update-slice_fusion.refs_11_), channel_id=1, source_target_pairs={{0,16},{16,0},{1,17},{17,1},{2,18},{18,2},{3,19},{19,3},{4,20},{20... | collective-permute-start | bytes 2359304 | tf_op jit(solution)/shard_map/ppermute | solution.py:38
  37.9 5.0 %collective-permute-start.16 = (bf16[2,128,768]{2,1,0:T(8,128)(2,1)S(1)}, bf16[2,128,768]{2,1,0:T(8,128)(2,1)S(1)}, u32[]{:S(2)}, u32[]{:S(2)}) collective-permute-start(bf16[2,128,768]{2,1,0:T(8,128)(2,1)S(1)} %collective-permute-done.10.refs_12_), channel_id=1, source_target_pairs={{0,8},{8,0},{1,9},{9,1},{2,10},{10,2},{3,11},{11,3},{4,12},{12,4},... | collective-permute-start | bytes 1179656 | tf_op jit(solution)/shard_map/ppermute | solution.py:38
  40.2 18.3 %collective-permute-start.4 = (bf16[384,768]{1,0:T(8,128)(2,1)S(1)}, bf16[384,768]{1,0:T(8,128)(2,1)}, u32[]{:S(2)}, u32[]{:S(2)}) collective-permute-start(bf16[384,768]{1,0:T(8,128)(2,1)S(1)} %broadcast_select_fusion), channel_id=1, source_target_pairs={{0,2},{1,3},{2,0},{3,1},{4,6},{5,7},{6,4},{7,5},{8,10},{9,11},{10,... | collective-permute-start | bytes 1769480 | tf_op jit(solution)/shard_map/ppermute | solution.py:38
  43.7 21.2 %collective-permute-start.15 = (bf16[2,256,768]{2,1,0:T(8,128)(2,1)S(1)}, bf16[2,256,768]{2,1,0:T(8,128)(2,1)S(1)}, u32[]{:S(2)}, u32[]{:S(2)}) collective-permute-start(bf16[2,256,768]{2,1,0:T(8,128)(2,1)S(1)} %constant_dynamic-update-slice_fusion.refs_11_), channel_id=1, source_target_pairs={{0,8},{8,0},{1,9},{9,1},{2,10},{10,2},{3,11},{11,3},{4,12},{12,4},... | collective-permute-start | bytes 2359304 | tf_op jit(solution)/shard_map/ppermute | solution.py:38
  45.3 18.3 %collective-permute-start.3 = (bf16[384,768]{1,0:T(8,128)(2,1)S(1)}, bf16[384,768]{1,0:T(8,128)(2,1)}, u32[]{:S(2)}, u32[]{:S(2)}) collective-permute-start(bf16[384,768]{1,0:T(8,128)(2,1)S(1)} %collective-permute-done.1.refs_3_), channel_id=1, source_target_pairs={{0,1},{1,2},{2,3},{3,0},{8,11},{9,8},{10,9},{11,10},{4,5},{5,6},{6... | collective-permute-start | bytes 1769480 | tf_op jit(solution)/shard_map/ppermute | solution.py:238
  49.4 14.5 %collective-permute-start.5 = (bf16[384,768]{1,0:T(8,128)(2,1)}, bf16[384,768]{1,0:T(8,128)(2,1)S(1)}, u32[]{:S(2)}, u32[]{:S(2)}) collective-permute-start(bf16[384,768]{1,0:T(8,128)(2,1)} %collective-permute-done.2.refs_4_), channel_id=1, source_target_pairs={{0,8},{8,0},{1,9},{9,1},{2,10},{10,2},{3,11},{11,3},{4,12},{12,4},... | collective-permute-start | bytes 1769480 | tf_op jit(solution)/shard_map/ppermute | solution.py:38
  57.6 10.2 %collective-permute-start.18 = (bf16[2,256,768]{2,1,0:T(8,128)(2,1)S(1)}, bf16[2,256,768]{2,1,0:T(8,128)(2,1)}, u32[]{:S(2)}, u32[]{:S(2)}) collective-permute-start(bf16[2,256,768]{2,1,0:T(8,128)(2,1)S(1)} %collective-permute-done.12.refs_14_), channel_id=1, source_target_pairs={{0,8},{8,0},{1,9},{9,1},{2,10},{10,2},{3,11},{11,3},{4,12},{12,4},... | collective-permute-start | bytes 2359304 | tf_op jit(solution)/shard_map/ppermute | solution.py:38
  58.5 32.9 %collective-permute-start = (bf16[128,3072]{1,0:T(8,128)(2,1)}, bf16[128,3072]{1,0:T(8,128)(2,1)}, u32[]{:S(2)}, u32[]{:S(2)}) collective-permute-start(bf16[128,3072]{1,0:T(8,128)(2,1)} %bitcast.9.refs_1_), channel_id=1, source_target_pairs={{0,64},{32,96},{64,0},{96,32},{1,65},{33,97},{65,1},{97,33},{2,66}... | collective-permute-start | bytes 2359304 | tf_op jit(solution)/shard_map/ppermute | solution.py:38
  63.6 4.3 %collective-permute-start.7 = (bf16[384,768]{1,0:T(8,128)(2,1)}, bf16[384,768]{1,0:T(8,128)(2,1)}, u32[]{:S(2)}, u32[]{:S(2)}) collective-permute-start(bf16[384,768]{1,0:T(8,128)(2,1)} %collective-permute-done.4.refs_6_), channel_id=1, source_target_pairs={{0,8},{8,0},{1,9},{9,1},{2,10},{10,2},{3,11},{11,3},{4,12},{12,4},... | collective-permute-start | bytes 1769480 | tf_op jit(solution)/shard_map/ppermute | solution.py:38
  64.7 3.2 %collective-permute-start.6 = (bf16[384,768]{1,0:T(8,128)(2,1)}, bf16[384,768]{1,0:T(8,128)(2,1)}, u32[]{:S(2)}, u32[]{:S(2)}) collective-permute-start(bf16[384,768]{1,0:T(8,128)(2,1)} %collective-permute-done.3.refs_5_), channel_id=1, source_target_pairs={{0,8},{8,0},{1,9},{9,1},{2,10},{10,2},{3,11},{11,3},{4,12},{12,4},... | collective-permute-start | bytes 1769480 | tf_op jit(solution)/shard_map/ppermute | solution.py:38
  87.9 19.3 %collective-permute-start.22 = (bf16[128,768]{1,0:T(8,128)(2,1)S(1)}, bf16[128,768]{1,0:T(8,128)(2,1)S(1)}, u32[]{:S(2)}, u32[]{:S(2)}) collective-permute-start(bf16[128,768]{1,0:T(8,128)(2,1)S(1)} %get-tuple-element.18), channel_id=1, source_target_pairs={{0,96},{32,0},{64,32},{96,64},{1,97},{33,1},{65,33},{97,65},{2,98}... | collective-permute-start | bytes 589832 | tf_op jit(solution)/shard_map/ppermute | solution.py:38
  91.4 16.6 %collective-permute-start.23 = (bf16[128,768]{1,0:T(8,128)(2,1)S(1)}, bf16[128,768]{1,0:T(8,128)(2,1)S(1)}, u32[]{:S(2)}, u32[]{:S(2)}) collective-permute-start(bf16[128,768]{1,0:T(8,128)(2,1)S(1)} %get-tuple-element.19), channel_id=1, source_target_pairs={{0,32},{32,64},{64,96},{96,0},{1,33},{33,65},{65,97},{97,1},{2,34}... | collective-permute-start | bytes 589832 | tf_op jit(solution)/shard_map/ppermute | solution.py:38
  105.8 7.3 %collective-permute-start.24 = (bf16[128,768]{1,0:T(8,128)(2,1)S(1)}, bf16[128,768]{1,0:T(8,128)(2,1)S(1)}, u32[]{:S(2)}, u32[]{:S(2)}) collective-permute-start(bf16[128,768]{1,0:T(8,128)(2,1)S(1)} %get-tuple-element.20), channel_id=1, source_target_pairs={{0,64},{32,96},{64,0},{96,32},{1,65},{33,97},{65,1},{97,33},{2,66}... | collective-permute-start | bytes 589832 | tf_op jit(solution)/shard_map/ppermute | solution.py:38
  (24 other events, 107.9 us)
